TPU v7x, 16 devices: a whole 2x2x2 slice. The times are simulated.
16 devices in a mesh: fsdp: 16 (over z, y, x, core).
Axes of the slice: x: 2, y: 2, z: 2, core: 2. Of those that a mesh axis runs over, the one named last changes fastest.
Arguments:
- x_saved: bfloat16 [2, 2, 16, 1024, 1024], P(None, None, 'fsdp')
- grad_out: bfloat16 [2, 16, 1024, 1024], P(None, 'fsdp')
- x_next: bfloat16 [2, 16, 1024, 1024], P(None, 'fsdp')
- w_up: bfloat16 [2, 2, 1024, 4096], replicated
- w_down: bfloat16 [2, 2, 4096, 1024], replicated
- acc_up: float32 [2, 2, 1024, 4096], P(None, None, 'fsdp')
- acc_down: float32 [2, 2, 4096, 1024], P(None, None, 'fsdp')
- master_up: float32 [2, 2, 1024, 4096], P(None, None, 'fsdp')
- master_down: float32 [2, 2, 4096, 1024], P(None, None, 'fsdp')
- moment1_up: float32 [2, 2, 1024, 4096], P(None, None, 'fsdp')
- moment1_down: float32 [2, 2, 4096, 1024], P(None, None, 'fsdp')
- moment2_up: float32 [2, 2, 1024, 4096], P(None, None, 'fsdp')
- moment2_down: float32 [2, 2, 4096, 1024], P(None, None, 'fsdp')
Outputs:
- output 1: float32 [2, 2, 1024, 4096], P(None, None, 'fsdp')
- output 2: float32 [2, 2, 4096, 1024], P(None, None, 'fsdp')
- output 3: float32 [2, 2, 1024, 4096], P(None, None, 'fsdp')
- output 4: float32 [2, 2, 4096, 1024], P(None, None, 'fsdp')
- output 5: float32 [2, 2, 1024, 4096], P(None, None, 'fsdp')
- output 6: float32 [2, 2, 4096, 1024], P(None, None, 'fsdp')
- output 7: bfloat16 [2, 16, 1024, 1024], P(None, 'fsdp')
All inputs are finite; a program needn't handle non-finite values.
Results may differ from a plain program's by a relative error of at most 0.00724236.
Values are sent between devices in bfloat16 or wider.
A program may use at most 1 GiB of HBM per device.

v0:
```python
import jax
import jax.numpy as jnp
from jax import lax
from jax.sharding import PartitionSpec as P

LEARN_RATE = 0.005
BETA_ONE = 0.9
BETA_TWO = 0.95
ADAM_EPS = 1e-8
WEIGHT_DECAY = 0.1
MICROBATCHES = 2
ADAM_STEP = 2


def adam_update(acc_part, grad_new, master, moment_one, moment_two):
    grad_mean = (acc_part + grad_new) / MICROBATCHES
    moment_one = BETA_ONE * moment_one + (1.0 - BETA_ONE) * grad_mean
    moment_two = BETA_TWO * moment_two + (1.0 - BETA_TWO) * grad_mean * grad_mean
    corr_one = 1.0 - BETA_ONE ** ADAM_STEP
    corr_two = 1.0 - BETA_TWO ** ADAM_STEP
    step_dir = (moment_one / corr_one) / (jnp.sqrt(moment_two / corr_two) + ADAM_EPS)
    master = master - LEARN_RATE * (step_dir + WEIGHT_DECAY * master)
    return master, moment_one, moment_two


def backward_layer(x_in, cotangent, w_one, w_two):
    hidden = jnp.einsum('bsd,df->bsf', x_in, w_one, preferred_element_type=jnp.float32)
    gelu_out, gelu_vjp = jax.vjp(jax.nn.gelu, hidden)
    grad_act = jnp.einsum('bsd,fd->bsf', cotangent, w_two, preferred_element_type=jnp.float32)
    grad_hidden = gelu_vjp(grad_act)[0].astype(jnp.bfloat16)
    part_down = jnp.einsum('bsf,bsd->fd', gelu_out.astype(jnp.bfloat16), cotangent, preferred_element_type=jnp.float32)
    part_up = jnp.einsum('bsd,bsf->df', x_in, grad_hidden, preferred_element_type=jnp.float32)
    return part_up, part_down, grad_hidden


def forward_layer(x_in, w_one, w_two):
    hidden = jnp.einsum('bsd,df->bsf', x_in, w_one, preferred_element_type=jnp.float32)
    gelu_out = jax.nn.gelu(hidden).astype(jnp.bfloat16)
    mlp_val = jnp.einsum('bsf,fd->bsd', gelu_out, w_two, preferred_element_type=jnp.float32)
    return (x_in.astype(jnp.float32) + mlp_val).astype(jnp.bfloat16)


def scatter_sum(part, groups):
    received = lax.all_to_all(part.astype(jnp.bfloat16), 'fsdp', 0, 0, tiled=True)
    return jnp.sum(received.reshape((groups, -1) + received.shape[1:]), axis=0, dtype=jnp.float32)


def solution(mesh):
    groups = mesh.shape['fsdp']
    tok_spec = P(None, 'fsdp')
    layer_spec = P(None, None, 'fsdp')
    rep_spec = P()

    def device_step(x_saved, grad_out, x_next, w_up, w_down, acc_up, acc_down, master_up, master_down, moment1_up, moment1_down, moment2_up, moment2_down):
        stages = x_saved.shape[0]
        layers = x_saved.shape[1]
        state_lists = [[], [], [], [], [], []]
        y_list = []
        for stage_id in range(stages):
            cotangent = grad_out[stage_id]
            stage_state = [[None] * layers for state_id in range(6)]
            full_up = [None] * layers
            full_down = [None] * layers
            for layer_id in reversed(range(layers)):
                cur_up = w_up[stage_id, layer_id]
                cur_down = w_down[stage_id, layer_id]
                part_up, part_down, grad_hidden = backward_layer(x_saved[stage_id, layer_id], cotangent, cur_up, cur_down)
                if layer_id > 0:
                    cotangent = (cotangent.astype(jnp.float32) + jnp.einsum('bsf,df->bsd', grad_hidden, cur_up, preferred_element_type=jnp.float32)).astype(jnp.bfloat16)
                sum_up = scatter_sum(part_up, groups)
                sum_down = scatter_sum(part_down, groups)
                new_up = adam_update(acc_up[stage_id, layer_id], sum_up, master_up[stage_id, layer_id], moment1_up[stage_id, layer_id], moment2_up[stage_id, layer_id])
                new_down = adam_update(acc_down[stage_id, layer_id], sum_down, master_down[stage_id, layer_id], moment1_down[stage_id, layer_id], moment2_down[stage_id, layer_id])
                for state_id in range(3):
                    stage_state[2 * state_id][layer_id] = new_up[state_id]
                    stage_state[2 * state_id + 1][layer_id] = new_down[state_id]
                full_up[layer_id] = lax.all_gather(new_up[0].astype(jnp.bfloat16), 'fsdp', axis=0, tiled=True)
                full_down[layer_id] = lax.all_gather(new_down[0].astype(jnp.bfloat16), 'fsdp', axis=0, tiled=True)
            hidden_x = x_next[stage_id]
            for layer_id in range(layers):
                hidden_x = forward_layer(hidden_x, full_up[layer_id], full_down[layer_id])
            y_list.append(hidden_x)
            for state_id in range(6):
                state_lists[state_id].append(jnp.stack(stage_state[state_id]))
        return tuple(jnp.stack(entry) for entry in state_lists) + (jnp.stack(y_list),)

    return jax.shard_map(device_step, mesh=mesh, in_specs=(layer_spec, tok_spec, tok_spec, rep_spec, rep_spec) + (layer_spec,) * 8, out_specs=(layer_spec,) * 6 + (tok_spec,), check_vma=False)
```

profile of v0, /device:TPU:0, one launch (start us, length us, event | category | flops | bytes accessed | tf_op | source)
XLA Modules:
  0.0 1271.6 jit_solution(8138367371094024077)
XLA Ops:
  7.2 16.2 %fusion.82 = f32[1024,4096]{1,0:T(8,128)} fusion(bf16[2,2,1024,4096]{3,2,1,0:T(8,128)(2,1)} %param.16, bf16[2,2,1,1024,1024]{4,3,2,1,0:T(8,128)(2,1)} %param.13), kind=kOutput, calls=%fused_computation.106 | convolution fusion | flops 8589934592 | bytes 27262976 | tf_op jit(solution)/shard_map/bsd,df->bsf/dot_general | solution.py:27
  23.3 17.3 %fusion.132 = bf16[4096,1024]{1,0:T(8,128)(2,1)} fusion(f32[1024,4096]{1,0:T(8,128)} %fusion.82, bf16[2,1,1024,1024]{3,2,1,0:T(8,128)(2,1)S(1)} %copy-done.33), kind=kOutput, calls=%fused_computation.150 | convolution fusion | flops 8631877632 | bytes 27262976 | tf_op jit(solution)/shard_map/bsf,bsd->fd/dot_general | solution.py:31
  46.2 24.6 %fusion.6 = bf16[1024,4096]{1,0:T(8,128)(2,1)} fusion(f32[1024,4096]{1,0:T(8,128)} %fusion.82, bf16[2,2,4096,1024]{3,2,1,0:T(8,128)(2,1)} %param.17, bf16[2,1,1024,1024]{3,2,1,0:T(8,128)(2,1)} %param.14), kind=kOutput, calls=%fused_computation.18 | convolution fusion | flops 8673820672 | bytes 35651584 | tf_op jit(solution)/shard_map/bsd,fd->bsf/dot_general | solution.py:29
  86.0 16.2 %fusion.76 = f32[1024,4096]{1,0:T(8,128)} fusion(bf16[2,2,1024,4096]{3,2,1,0:T(8,128)(2,1)} %param.16, bf16[2,2,1,1024,1024]{4,3,2,1,0:T(8,128)(2,1)} %param.13), kind=kOutput, calls=%fused_computation.100 | convolution fusion | flops 8589934592 | bytes 27262976 | tf_op jit(solution)/shard_map/bsd,df->bsf/dot_general | solution.py:27
  130.0 23.1 %all-to-all-done.5 = bf16[16,256,1024]{2,1,0:T(8,128)(2,1)} async-done(((bf16[16,256,1024]{2,1,0:T(8,128)(2,1)}), bf16[16,256,1024]{2,1,0:T(8,128)(2,1)}, u32[]{:S(2)}, u32[]{:S(2)}) %all-to-all-start.5) | async-done | bytes 8388640 | tf_op jit(solution)/shard_map/all_to_all | solution.py:44
  157.1 24.7 %fusion.20 = bf16[1024,4096]{1,0:T(8,128)(2,1)} fusion(f32[1024,4096]{1,0:T(8,128)} %fusion.72, bf16[2,2,4096,1024]{3,2,1,0:T(8,128)(2,1)} %param.17, bf16[2,1,1024,1024]{3,2,1,0:T(8,128)(2,1)} %param.14), kind=kOutput, calls=%fused_computation.32 | convolution fusion | flops 8673820672 | bytes 35651584 | tf_op jit(solution)/shard_map/bsd,fd->bsf/dot_general | solution.py:29
  181.8 28.2 %fusion.124 = bf16[4096,1024]{0,1:T(8,128)(2,1)} fusion(f32[1024,4096]{1,0:T(8,128)} %fusion.76, bf16[1024,1024]{1,0:T(8,128)(2,1)S(1)} %add_convert_fusion.5, bf16[2,2,4096,1024]{3,2,1,0:T(8,128)(2,1)} %param.17, bf16[2,2,1,1024,1024]{4,3,2,1,0:T(8,128)(2,1)} %param.13), kind=kOutput, calls=%fused_computation.144 | convolution fusion | flops 17267949568 | bytes 37748736 | tf_op jit(solution)/shard_map/bsd,bsf->df/dot_general | solution.py:32
  210.0 54.1 %all-to-all-done.1 = bf16[16,64,4096]{2,1,0:T(8,128)(2,1)} async-done(((bf16[16,64,4096]{2,1,0:T(8,128)(2,1)}), bf16[16,64,4096]{2,1,0:T(8,128)(2,1)}, u32[]{:S(2)}, u32[]{:S(2)}) %all-to-all-start.1) | async-done | bytes 8388640 | tf_op jit(solution)/shard_map/all_to_all | solution.py:44
  298.2 28.8 %fusion.127 = bf16[4096,1024]{0,1:T(8,128)(2,1)} fusion(f32[1024,4096]{1,0:T(8,128)} %fusion.66, bf16[1024,1024]{1,0:T(8,128)(2,1)S(1)} %add_convert_fusion.4, bf16[2,2,4096,1024]{3,2,1,0:T(8,128)(2,1)} %param.17, bf16[2,2,1,1024,1024]{4,3,2,1,0:T(8,128)(2,1)} %param.13), kind=kOutput, calls=%fused_computation.145 | convolution fusion | flops 17267949568 | bytes 37748736 | tf_op jit(solution)/shard_map/bsd,bsf->df/dot_general | solution.py:32
  327.0 48.2 %all-to-all-done = bf16[16,64,4096]{2,1,0:T(8,128)(2,1)} async-done(((bf16[16,64,4096]{2,1,0:T(8,128)(2,1)}), bf16[16,64,4096]{2,1,0:T(8,128)(2,1)}, u32[]{:S(2)}, u32[]{:S(2)}) %all-to-all-start) | async-done | bytes 8388640 | tf_op jit(solution)/shard_map/all_to_all | solution.py:44
  379.7 17.3 %fusion.133 = bf16[4096,1024]{1,0:T(8,128)(2,1)} fusion(bf16[1024,1024]{1,0:T(8,128)(2,1)S(1)} %copy-done.38, f32[1024,4096]{1,0:T(8,128)} %fusion.76), kind=kOutput, calls=%fused_computation.151 | convolution fusion | flops 8631877632 | bytes 27262976 | tf_op jit(solution)/shard_map/bsf,bsd->fd/dot_general | solution.py:31
  407.0 79.6 %all-to-all-done.2 = bf16[16,64,4096]{2,1,0:T(8,128)(2,1)} async-done(((bf16[16,64,4096]{2,1,0:T(8,128)(2,1)}), bf16[16,64,4096]{2,1,0:T(8,128)(2,1)}, u32[]{:S(2)}, u32[]{:S(2)}) %all-to-all-start.2) | async-done | bytes 8388640 | tf_op jit(solution)/shard_map/all_to_all | solution.py:44
  502.2 17.9 %fusion.131 = bf16[4096,1024]{1,0:T(8,128)(2,1)} fusion(bf16[1024,1024]{1,0:T(8,128)(2,1)} %copy-done.36, f32[1024,4096]{1,0:T(8,128)} %fusion.66), kind=kOutput, calls=%fused_computation.149 | convolution fusion | flops 8631877632 | bytes 27262976 | tf_op jit(solution)/shard_map/bsf,bsd->fd/dot_general | solution.py:31
  520.1 91.2 %all-to-all-done.4 = bf16[16,256,1024]{2,1,0:T(8,128)(2,1)} async-done(((bf16[16,256,1024]{2,1,0:T(8,128)(2,1)}), bf16[16,256,1024]{2,1,0:T(8,128)(2,1)}, u32[]{:S(2)}, u32[]{:S(2)}) %all-to-all-start.4) | async-done | bytes 8388640 | tf_op jit(solution)/shard_map/all_to_all | solution.py:44
  628.1 89.1 %all-to-all-done.6 = bf16[16,256,1024]{2,1,0:T(8,128)(2,1)} async-done(((bf16[16,256,1024]{2,1,0:T(8,128)(2,1)}), bf16[16,256,1024]{2,1,0:T(8,128)(2,1)}, u32[]{:S(2)}, u32[]{:S(2)}) %all-to-all-start.6) | async-done | bytes 8388640 | tf_op jit(solution)/shard_map/all_to_all | solution.py:44
  747.8 119.6 %all_to_all.72 = bf16[16,256,1024]{2,1,0:T(8,128)(2,1)S(1)} all-to-all(bf16[16,256,1024]{2,1,0:T(8,128)(2,1)S(1)} %bitcast.725), channel_id=1, replica_groups=mesh['fsdp'=16] {'fsdp'}, dimensions={0} | all-to-all | bytes 16777216 | tf_op jit(solution)/shard_map/all_to_all | solution.py:44
  897.9 111.6 %all-to-all-done.3 = bf16[16,64,4096]{2,1,0:T(8,128)(2,1)} async-done(((bf16[16,64,4096]{2,1,0:T(8,128)(2,1)}), bf16[16,64,4096]{2,1,0:T(8,128)(2,1)}, u32[]{:S(2)}, u32[]{:S(2)}) %all-to-all-start.3) | async-done | bytes 8388640 | tf_op jit(solution)/shard_map/all_to_all | solution.py:44
  1059.4 26.4 %add_convert_fusion.3 = bf16[1024,1024]{1,0:T(8,128)(2,1)} fusion(bf16[4096,1024]{1,0:T(8,128)(2,1)} %all-gather.11.cloned.1.call-done, bf16[1024,4096]{1,0:T(8,128)(2,1)} %all-gather.9.cloned.1.call-done, bf16[2,1,1024,1024]{3,2,1,0:T(8,128)(2,1)} %param.15), kind=kOutput, calls=%fused_computation.166 | convolution fusion | flops 17220763648 | bytes 23068672 | tf_op jit(solution)/shard_map/bsf,fd->bsd/dot_general | solution.py:39
  1085.8 26.2 %add_convert_fusion.1 = bf16[1024,1024]{1,0:T(8,128)(2,1)} fusion(bf16[4096,1024]{1,0:T(8,128)(2,1)} %all-gather.19.cloned.1.call-done, bf16[1024,4096]{1,0:T(8,128)(2,1)} %all-gather.17.cloned.1.call-done, bf16[2,1,1024,1024]{3,2,1,0:T(8,128)(2,1)} %param.15), kind=kOutput, calls=%fused_computation.164 | convolution fusion | flops 17220763648 | bytes 23068672 | tf_op jit(solution)/shard_map/bsf,fd->bsd/dot_general | solution.py:39
  1111.9 20.3 %all-gather.15.cloned.1.call-done = bf16[4096,1024]{1,0:T(8,128)(2,1)} async-done(((bf16[256,1024]{1,0:T(8,128)(2,1)}), bf16[4096,1024]{1,0:T(8,128)(2,1)}) %all-gather.15.cloned.1.call-update) | async-done | bytes 8388624 | tf_op jit(solution)/shard_map/all_gather | solution.py:78
  1132.3 24.8 %fusion.154 = bf16[1,1,1024,1024]{3,2,1,0:T(8,128)(2,1)S(1)} fusion(bf16[1024,1024]{1,0:T(8,128)(2,1)} %add_convert_fusion.3, bf16[4096,1024]{1,0:T(8,128)(2,1)} %all-gather.15.cloned.1.call-done, bf16[1024,4096]{1,0:T(8,128)(2,1)} %all-gather.13.cloned.1.call-done), kind=kOutput, calls=%fused_computation.169 | convolution fusion | flops 17220763648 | bytes 20971520 | tf_op jit(solution)/shard_map/bsf,fd->bsd/dot_general | solution.py:39
  1157.1 26.1 %all-gather.23.cloned.1.call-done = bf16[4096,1024]{1,0:T(8,128)(2,1)} async-done(((bf16[256,1024]{1,0:T(8,128)(2,1)}), bf16[4096,1024]{1,0:T(8,128)(2,1)}) %all-gather.23.cloned.1.call-update) | async-done | bytes 8388624 | tf_op jit(solution)/shard_map/all_gather | solution.py:78
  1183.2 50.9 %all-gather.21.cloned.1.call-done = bf16[1024,4096]{1,0:T(8,128)(2,1)} async-done(((bf16[64,4096]{1,0:T(8,128)(2,1)}), bf16[1024,4096]{1,0:T(8,128)(2,1)}) %all-gather.21.cloned.1.call-update) | async-done | bytes 8388624 | tf_op jit(solution)/shard_map/all_gather | solution.py:77
  1234.1 26.2 %fusion.155 = bf16[1,1,1024,1024]{3,2,1,0:T(8,128)(2,1)} fusion(bf16[1024,1024]{1,0:T(8,128)(2,1)} %add_convert_fusion.1, bf16[4096,1024]{1,0:T(8,128)(2,1)} %all-gather.23.cloned.1.call-done, bf16[1024,4096]{1,0:T(8,128)(2,1)} %all-gather.21.cloned.1.call-done), kind=kOutput, calls=%fused_computation.170 | convolution fusion | flops 17220763648 | bytes 20971520 | tf_op jit(solution)/shard_map/bsf,fd->bsd/dot_general | solution.py:39
  (147 shorter events, 248.0 us)
Async XLA Ops:
  7.2 16.2 %copy-start.33 = (bf16[2,1,1024,1024]{3,2,1,0:T(8,128)(2,1)S(1)}, bf16[2,1,1024,1024]{3,2,1,0:T(8,128)(2,1)}, u32[]{:S(2)}) copy-start(bf16[2,1,1024,1024]{3,2,1,0:T(8,128)(2,1)} %param.14) | copy-start | bytes 12582916
  40.7 112.4 %all-to-all-start.5 = ((bf16[16,256,1024]{2,1,0:T(8,128)(2,1)}), bf16[16,256,1024]{2,1,0:T(8,128)(2,1)}, u32[]{:S(2)}, u32[]{:S(2)}) async-start(bf16[16,256,1024]{2,1,0:T(8,128)(2,1)} %bitcast.724), calls=%async_computation.5 | async-start | bytes 16777216 | tf_op jit(solution)/shard_map/all_to_all | solution.py:44
  86.0 32.3 %slice-start = ((s8[8388608]{0:T(1024)(128)(4,1)}), s8[4194304]{0:T(1024)(128)(4,1)S(1)}, s32[]{:S(2)}) async-start(s8[8388608]{0:T(1024)(128)(4,1)} %bitcast.726), calls=%async_computation.16 | async-start | bytes 8388608
  102.1 16.2 %copy-start.34 = (bf16[2,1,1024,1024]{3,2,1,0:T(8,128)(2,1)S(1)}, bf16[2,1,1024,1024]{3,2,1,0:T(8,128)(2,1)}, u32[]{:S(2)}) copy-start(bf16[2,1,1024,1024]{3,2,1,0:T(8,128)(2,1)} %param.14) | copy-start | bytes 12582916
  102.1 16.2 %slice-start.1 = ((s8[8388608]{0:T(1024)(128)(4,1)}), s8[4194304]{0:T(1024)(128)(4,1)S(1)}, s32[]{:S(2)}) async-start(s8[8388608]{0:T(1024)(128)(4,1)} %bitcast.726), calls=%async_computation.17 | async-start | bytes 8388608
  130.0 51.8 %copy-start.37 = (bf16[1024,1024]{1,0:T(8,128)(2,1)}, bf16[1024,1024]{1,0:T(8,128)(2,1)S(1)}, u32[]{:S(2)}) copy-start(bf16[1024,1024]{1,0:T(8,128)(2,1)S(1)} %add_convert_fusion.5) | copy-start | bytes 6291460
  153.1 110.9 %all-to-all-start.1 = ((bf16[16,64,4096]{2,1,0:T(8,128)(2,1)}), bf16[16,64,4096]{2,1,0:T(8,128)(2,1)}, u32[]{:S(2)}, u32[]{:S(2)}) async-start(bf16[16,64,4096]{2,1,0:T(8,128)(2,1)} %bitcast.721), calls=%async_computation.1 | async-start | bytes 16777216 | tf_op jit(solution)/shard_map/all_to_all | solution.py:44
  264.0 111.1 %all-to-all-start = ((bf16[16,64,4096]{2,1,0:T(8,128)(2,1)}), bf16[16,64,4096]{2,1,0:T(8,128)(2,1)}, u32[]{:S(2)}, u32[]{:S(2)}) async-start(bf16[16,64,4096]{2,1,0:T(8,128)(2,1)} %bitcast.722), calls=%async_computation | async-start | bytes 16777216 | tf_op jit(solution)/shard_map/all_to_all | solution.py:44
  268.3 16.1 %copy-start.35 = (bf16[2,1,1024,1024]{3,2,1,0:T(8,128)(2,1)S(1)}, bf16[2,1,1024,1024]{3,2,1,0:T(8,128)(2,1)}, u32[]{:S(2)}) copy-start(bf16[2,1,1024,1024]{3,2,1,0:T(8,128)(2,1)} %param.14) | copy-start | bytes 12582916
  298.2 28.8 %copy-start.36 = (bf16[1024,1024]{1,0:T(8,128)(2,1)}, bf16[1024,1024]{1,0:T(8,128)(2,1)S(1)}, u32[]{:S(2)}) copy-start(bf16[1024,1024]{1,0:T(8,128)(2,1)S(1)} %add_convert_fusion.4) | copy-start | bytes 6291460
  375.2 111.4 %all-to-all-start.2 = ((bf16[16,64,4096]{2,1,0:T(8,128)(2,1)}), bf16[16,64,4096]{2,1,0:T(8,128)(2,1)}, u32[]{:S(2)}, u32[]{:S(2)}) async-start(bf16[16,64,4096]{2,1,0:T(8,128)(2,1)} %bitcast.720), calls=%async_computation.2 | async-start | bytes 16777216 | tf_op jit(solution)/shard_map/all_to_all | solution.py:44
  486.6 124.8 %all-to-all-start.4 = ((bf16[16,256,1024]{2,1,0:T(8,128)(2,1)}), bf16[16,256,1024]{2,1,0:T(8,128)(2,1)}, u32[]{:S(2)}, u32[]{:S(2)}) async-start(bf16[16,256,1024]{2,1,0:T(8,128)(2,1)} %bitcast.718), calls=%async_computation.4 | async-start | bytes 16777216 | tf_op jit(solution)/shard_map/all_to_all | solution.py:44
  490.6 568.8 %all-gather.9.cloned.1.call-start = ((), (), s32[]{:S(2)}) async-start(), calls=%async_computation.8 | async-start | bytes 8912896 | tf_op jit(solution)/shard_map/all_gather | solution.py:77
  611.3 105.8 %all-to-all-start.6 = ((bf16[16,256,1024]{2,1,0:T(8,128)(2,1)}), bf16[16,256,1024]{2,1,0:T(8,128)(2,1)}, u32[]{:S(2)}, u32[]{:S(2)}) async-start(bf16[16,256,1024]{2,1,0:T(8,128)(2,1)} %bitcast.719), calls=%async_computation.6 | async-start | bytes 16777216 | tf_op jit(solution)/shard_map/all_to_all | solution.py:44
  615.9 443.5 %all-gather.11.cloned.1.call-start = ((), (), s32[]{:S(2)}) async-start(), calls=%async_computation.9 | async-start | bytes 8912896 | tf_op jit(solution)/shard_map/all_gather | solution.py:78
  729.0 356.8 %all-gather.17.cloned.1.call-start = ((), (), s32[]{:S(2)}) async-start(), calls=%async_computation.12 | async-start | bytes 8912896 | tf_op jit(solution)/shard_map/all_gather | solution.py:77
  729.7 356.0 %all-gather.19.cloned.1.call-start = ((), (), s32[]{:S(2)}) async-start(), calls=%async_computation.13 | async-start | bytes 8912896 | tf_op jit(solution)/shard_map/all_gather | solution.py:78
  730.3 381.6 %all-gather.13.cloned.1.call-start = ((), (), s32[]{:S(2)}) async-start(), calls=%async_computation.10 | async-start | bytes 8912896 | tf_op jit(solution)/shard_map/all_gather | solution.py:77
  730.9 401.4 %all-gather.15.cloned.1.call-start = ((), (), s32[]{:S(2)}) async-start(), calls=%async_computation.11 | async-start | bytes 8912896 | tf_op jit(solution)/shard_map/all_gather | solution.py:78
  731.5 451.7 %all-gather.23.cloned.1.call-start = ((), (), s32[]{:S(2)}) async-start(), calls=%async_computation.15 | async-start | bytes 8912896 | tf_op jit(solution)/shard_map/all_gather | solution.py:78
  889.2 120.4 %all-to-all-start.3 = ((bf16[16,64,4096]{2,1,0:T(8,128)(2,1)}), bf16[16,64,4096]{2,1,0:T(8,128)(2,1)}, u32[]{:S(2)}, u32[]{:S(2)}) async-start(bf16[16,64,4096]{2,1,0:T(8,128)(2,1)} %bitcast.723), calls=%async_computation.3 | async-start | bytes 16777216 | tf_op jit(solution)/shard_map/all_to_all | solution.py:44
  892.7 341.4 %all-gather.21.cloned.1.call-start = ((), (), s32[]{:S(2)}) async-start(), calls=%async_computation.14 | async-start | bytes 8912896 | tf_op jit(solution)/shard_map/all_gather | solution.py:77
  1015.6 7.1 copy-start.11
  1026.6 6.2 copy-start.7
  (32 other events, 131.5 us)
Sparse Core Ops, SparseCore 0:
  502.3 119.5 all-gather.8
  729.1 113.2 all-gather.10
  844.7 84.2 all-gather.16
  931.1 99.5 all-gather.18
  1032.8 48.6 all-gather.12
  1083.6 48.6 all-gather.14
  1134.5 48.6 all-gather.22
  1185.4 48.6 all-gather.20
where the time goes:
time: 1280 us; the launch traced here: 1270 us
  waiting for transfers between devices  597 us (47%)
  matrix products  398 us (31%)
  blocking collectives  120 us (9%)
  other arithmetic  106 us (8%)
  starting transfers between devices  31.2 us (2%)
  between operations  15.1 us (1%)
    all_to_all x7, waiting for transfers between devices, scatter_sum(): lax.all_to_all(part.astype(jnp.bfloat16), 'fsdp', 0, 0, tiled=True)  497 us
    all_to_all x1, blocking collectives, scatter_sum(): lax.all_to_all(part.astype(jnp.bfloat16), 'fsdp', 0, 0, tiled=True)  120 us
    dot_general x4, matrix products, forward_layer(): jnp.einsum('bsf,fd->bsd', gelu_out, w_two, preferred_element_type=jnp.flo...  104 us
    dot_general x4, matrix products, backward_layer(): jnp.einsum('bsd,bsf->df', x_in, grad_hidden, preferred_element_type=jnp.f...  87 us
    dot_general x4, matrix products, backward_layer(): jnp.einsum('bsf,bsd->fd', gelu_out.astype(jnp.bfloat16), cotangent, prefe...  68.5 us
    dot_general x4, matrix products, backward_layer(): jnp.einsum('bsd,df->bsf', x_in, w_one, preferred_element_type=jnp.float32)  64.6 us
    all_gather x4, waiting for transfers between devices, device_step(): lax.all_gather(new_up[0].astype(jnp.bfloat16), 'fsdp', axis=0, tiled=True)  50.9 us
    dot_general x2, matrix products, backward_layer(): jnp.einsum('bsd,fd->bsf', cotangent, w_two, preferred_element_type=jnp.fl...  49.3 us
  transfers between devices with their start and end apart: 15, of which 10 were waited for; matrix products, arithmetic and copies ran while one was open for 35% of the time, Pallas kernels for 0%

commit v1 on v0

v1 whole, which is shorter than its diff:
```python
import jax
import jax.numpy as jnp
from jax import lax
from jax.sharding import Mesh, PartitionSpec as P

LEARN_RATE = 0.005
BETA_ONE = 0.9
BETA_TWO = 0.95
ADAM_EPS = 1e-8
WEIGHT_DECAY = 0.1
MICROBATCHES = 2
ADAM_STEP = 2
CORES = 2
SWAP = [(0, 1), (1, 0)]
F32 = jnp.float32
BF16 = jnp.bfloat16


def adam_update(acc_part, grad_new, master, moment_one, moment_two):
    grad_mean = (acc_part + grad_new) / MICROBATCHES
    moment_one = BETA_ONE * moment_one + (1.0 - BETA_ONE) * grad_mean
    moment_two = BETA_TWO * moment_two + (1.0 - BETA_TWO) * grad_mean * grad_mean
    corr_one = 1.0 - BETA_ONE ** ADAM_STEP
    corr_two = 1.0 - BETA_TWO ** ADAM_STEP
    step_dir = (moment_one / corr_one) / (jnp.sqrt(moment_two / corr_two) + ADAM_EPS)
    master = master - LEARN_RATE * (step_dir + WEIGHT_DECAY * master)
    return master, moment_one, moment_two


def swap(val):
    return lax.ppermute(val, 'core', SWAP)


def dot(a, b, ca, cb):
    return lax.dot_general(a, b, (((ca,), (cb,)), ((), ())), preferred_element_type=F32)


def pair(own):
    return jnp.concatenate([own, swap(own)], axis=0)


def scatter_sum(part, chips):
    part = part.astype(BF16).reshape((chips, -1) + part.shape[1:])
    received = lax.all_to_all(part, 'chip', 0, 0, tiled=True)
    return jnp.sum(received, axis=0, dtype=F32)


def solution(mesh):
    chips = mesh.shape['fsdp'] // CORES
    mesh2 = Mesh(mesh.devices.reshape(chips, CORES), ('chip', 'core'))
    both = ('chip', 'core')
    tok_spec = P(None, both)
    layer_spec = P(None, None, both)
    rep_spec = P()

    def device_step(x_saved, grad_out, x_next, w_up, w_down, acc_up, acc_down, master_up, master_down, moment1_up, moment1_down, moment2_up, moment2_down):
        stages, layers = x_saved.shape[:2]
        tokens, width = x_saved.shape[-2:]
        ff = w_up.shape[-1]
        half = ff // CORES
        blk = ff // (chips * CORES)
        core = lax.axis_index('core')

        def split_cols(w, which):
            return lax.dynamic_index_in_dim(w.reshape(w.shape[0], chips, CORES, blk), which, 2, keepdims=False).reshape(w.shape[0], half)

        def join_cols(low, high):
            rows = low.shape[0]
            return jnp.stack([low.reshape(rows, chips, blk), high.reshape(rows, chips, blk)], axis=2).reshape(rows, ff)

        state = [[[None] * layers for s in range(stages)] for i in range(6)]
        full_up = [[None] * layers for s in range(stages)]
        full_down = [[None] * layers for s in range(stages)]
        y_list = []
        for s in range(stages):
            own_cot = grad_out[s, 0]
            cot = pair(own_cot)
            for l in reversed(range(layers)):
                x = pair(x_saved[s, l, 0])
                w1 = split_cols(w_up[s, l], core)
                w2 = lax.dynamic_index_in_dim(w_down[s, l].reshape(chips, CORES, blk, width), core, 1, keepdims=False).reshape(half, width)
                hidden = dot(x, w1, 1, 0)
                gelu_out, gelu_vjp = jax.vjp(jax.nn.gelu, hidden)
                gelu_out = gelu_out.astype(BF16)
                part_down = dot(gelu_out, cot, 0, 0)
                sum_down = scatter_sum(part_down, chips)
                grad_act = dot(cot, w2, 1, 1)
                grad_hidden = gelu_vjp(grad_act)[0].astype(BF16)
                if l > 0:
                    back = dot(grad_hidden, w1, 1, 1)
                    own_cot = (own_cot.astype(F32) + back[:tokens] + swap(back[tokens:])).astype(BF16)
                    cot = pair(own_cot)
                part_up = dot(x, grad_hidden, 0, 0)
                sum_up = scatter_sum(part_up, chips)
                rows = sum_up.shape[0] // CORES
                mine = lax.dynamic_slice_in_dim(sum_up, core * rows, rows, 0)
                other = swap(lax.dynamic_slice_in_dim(sum_up, (1 - core) * rows, rows, 0))
                low = jnp.where(core == 0, mine, other)
                high = jnp.where(core == 0, other, mine)
                sum_up = join_cols(low, high)
                new_down = adam_update(acc_down[s, l], sum_down, master_down[s, l], moment1_down[s, l], moment2_down[s, l])
                new_up = adam_update(acc_up[s, l], sum_up, master_up[s, l], moment1_up[s, l], moment2_up[s, l])
                for i in range(3):
                    state[2 * i][s][l] = new_up[i]
                    state[2 * i + 1][s][l] = new_down[i]
                full_down[s][l] = lax.all_gather(new_down[0].astype(BF16), 'chip', axis=0, tiled=True)
                bf_up = new_up[0].astype(BF16)
                mine = split_cols(bf_up, core)
                other = swap(split_cols(bf_up, 1 - core))
                low = jnp.where(core == 0, mine, other)
                high = jnp.where(core == 0, other, mine)
                full_up[s][l] = lax.all_gather(jnp.concatenate([low, high], axis=0), 'chip', axis=0, tiled=True)
            own_x = x_next[s, 0]
            for l in range(layers):
                x = pair(own_x)
                hidden = dot(x, full_up[s][l], 1, 0)
                gelu_out = jax.nn.gelu(hidden).astype(BF16)
                mlp = dot(gelu_out, full_down[s][l], 1, 0)
                own_x = (own_x.astype(F32) + (mlp[:tokens] + swap(mlp[tokens:]))).astype(BF16)
            y_list.append(own_x)
        outs = tuple(jnp.stack([jnp.stack(per) for per in entry]) for entry in state)
        return outs + (jnp.stack(y_list)[:, None],)

    return jax.shard_map(device_step, mesh=mesh2, in_specs=(layer_spec, tok_spec, tok_spec, rep_spec, rep_spec) + (layer_spec,) * 8, out_specs=(layer_spec,) * 6 + (tok_spec,), check_vma=False)
```

time: 1280 us -> 1130 us (0.88)
  waiting for transfers between devices: 597 us -> 300 us
  local copies, waits for them, and re-layouts: 4.57 us -> 238 us
  blocking collectives: 120 us -> 0 us
  starting transfers between devices: 31.2 us -> 59.6 us
    all_to_all x7 -> x8, waiting for transfers between devices: 497 us -> 231 us  [scatter_sum(): received = lax.all_to_all(part, 'chip', 0, 0, tiled=True)]
    all_to_all x1 -> x0, blocking collectives: 120 us -> none  [scatter_sum(): lax.all_to_all(part.astype(jnp.bfloat16), 'fsdp', 0, 0, tiled=True)]
    slice x0 -> x10, local copies, waits for them, and re-layouts: none -> 71.5 us  [the longest x1 23 us: device_step(): w1 = split_cols(w_up[s, l], core)]
    unnamed x82 -> x166, local copies, waits for them, and re-layouts: 4.57 us -> 69.2 us
    dynamic_slice x0 -> x14, local copies, waits for them, and re-layouts: none -> 34.2 us  [the longest x4 16.7 us: device_step(): lax.dynamic_index_in_dim(w_down[s, l].reshape(chips, CORES, blk, width),...]
    all_gather x8, waiting for transfers between devices: 97.4 us -> 63.2 us  [the longest x4 49.2 us: device_step(): lax.all_gather(jnp.concatenate([low, high], axis=0), 'chip', axis=0, tile...]
    squeeze x0 -> x11, local copies, waits for them, and re-layouts: none -> 34.1 us  [the longest x4 11.3 us: device_step(): master_up[s, l]]
    all_to_all x7 -> x8, starting transfers between devices: 30.3 us -> 51.8 us  [scatter_sum(): received = lax.all_to_all(part, 'chip', 0, 0, tiled=True)]
  transfers between devices with their start and end apart: 15 -> 42, of which waited for: 10 -> 15; matrix products, arithmetic and copies ran while one was open for 35% -> 64% of each run, Pallas kernels for 0% -> 0%
where the time goes in v1:
time: 1130 us; the launch traced here: 1120 us
  matrix products  396 us (35%)
  waiting for transfers between devices  300 us (27%)
  local copies, waits for them, and re-layouts  238 us (21%)
  other arithmetic  114 us (10%)
  starting transfers between devices  59.6 us (5%)
  between operations  15.5 us (1%)
    dot_general x22, matrix products, dot(): lax.dot_general(a, b, (((ca,), (cb,)), ((), ())), preferred_element_type=...  396 us
    all_to_all x8, waiting for transfers between devices, scatter_sum(): received = lax.all_to_all(part, 'chip', 0, 0, tiled=True)  231 us
    unnamed x166, local copies, waits for them, and re-layouts  69.2 us
    all_to_all x8, starting transfers between devices, scatter_sum(): received = lax.all_to_all(part, 'chip', 0, 0, tiled=True)  51.8 us
    all_gather x4, waiting for transfers between devices, device_step(): lax.all_gather(jnp.concatenate([low, high], axis=0), 'chip', axis=0, tile...  49.2 us
    reduce_sum x8, other arithmetic, scatter_sum(): return jnp.sum(received, axis=0, dtype=F32)  26 us
    slice x1, local copies, waits for them, and re-layouts, device_step(): w1 = split_cols(w_up[s, l], core)  23 us
  transfers between devices with their start and end apart: 42, of which 15 were waited for; matrix products, arithmetic and copies ran while one was open for 64% of the time, Pallas kernels for 0%

profile of v1, /device:TPU:0, one launch (start us, length us, event | category | flops | bytes accessed | tf_op | source)
XLA Modules:
  0.0 1123.3 jit_solution(9256175169690829252)
XLA Ops:
  17.8 23.0 %fusion.297 = (bf16[1,1,1024,4096]{3,2,1,0:T(8,128)(2,1)}, bf16[1,1,1024,4096]{3,2,1,0:T(8,128)(2,1)}, bf16[1,1,1024,4096]{3,2,1,0:T(8,128)(2,1)}, bf16[1,1,1024,4096]{3,2,1,0:T(8,128)(2,1)}) fusion(bf16[2,2,1024,4096]{3,2,1,0:T(8,128)(2,1)} %param.16), kind=kLoop, calls=%fused_computation.466 | loop fusion | bytes 67108864 | tf_op jit(solution)/shard_map/slice | solution.py:80
  69.5 20.4 %fusion.296 = (bf16[1,1,4096,1024]{3,2,1,0:T(8,128)(2,1)}, bf16[1,1,4096,1024]{3,2,1,0:T(8,128)(2,1)}, bf16[1,1,4096,1024]{3,2,1,0:T(8,128)(2,1)}, bf16[1,1,4096,1024]{3,2,1,0:T(8,128)(2,1)S(1)}) fusion(bf16[2,2,4096,1024]{3,2,1,0:T(8,128)(2,1)} %param.17), kind=kLoop, calls=%fused_computation.465 | loop fusion | bytes 67108864 | tf_op jit(solution)/shard_map/slice | solution.py:81
  114.7 23.7 %fusion.6 = bf16[2048,2048]{1,0:T(8,128)(2,1)} fusion(f32[2048,2048]{1,0:T(8,128)} %fusion.135, bf16[2048,1024]{1,0:T(8,128)(2,1)S(1)} %bitcast.616, bf16[1024,1024]{1,0:T(8,128)(2,1)} %collective-permute-done.1, bf16[1024,1024]{1,0:T(8,128)(2,1)S(1)} %get-tuple-element.101), kind=kOutput, calls=%fused_computation.18 | convolution fusion | flops 8682209280 | bytes 33554432 | tf_op jit(solution)/shard_map/dot_general | solution.py:35
  169.3 23.2 %fusion.20 = bf16[2048,2048]{1,0:T(8,128)(2,1)} fusion(f32[2048,2048]{1,0:T(8,128)} %fusion.131, bf16[2048,1024]{1,0:T(8,128)(2,1)S(1)} %bitcast.608, bf16[1024,1024]{1,0:T(8,128)(2,1)} %collective-permute-done.8, bf16[1024,1024]{1,0:T(8,128)(2,1)} %get-tuple-element.102), kind=kOutput, calls=%fused_computation.32 | convolution fusion | flops 8682209280 | bytes 33554432 | tf_op jit(solution)/shard_map/dot_general | solution.py:35
  251.8 17.0 %fusion.122 = bf16[2048,1024]{1,0:T(8,128)(2,1)} fusion(f32[2048,2048]{1,0:T(8,128)} %fusion.135, bf16[1024,1024]{1,0:T(8,128)(2,1)} %collective-permute-done.1, bf16[1024,1024]{1,0:T(8,128)(2,1)S(1)} %copy-done.62), kind=kOutput, calls=%fused_computation.145 | convolution fusion | flops 8638169088 | bytes 25165824 | tf_op jit(solution)/shard_map/dot_general | solution.py:35
  275.0 15.3 %fusion.133 = f32[2048,2048]{1,0:T(8,128)} fusion(bf16[1024,2048]{0,1:T(8,128)(2,1)} %bitcast.603, bf16[1024,1024]{1,0:T(8,128)(2,1)} %collective-permute-done.7, bf16[1024,1024]{1,0:T(8,128)(2,1)} %get-tuple-element.78), kind=kOutput, calls=%fused_computation.154 | convolution fusion | flops 8598323200 | bytes 25165824 | tf_op jit(solution)/shard_map/dot_general | solution.py:35
  290.4 16.9 %fusion.121 = bf16[2048,1024]{1,0:T(8,128)(2,1)} fusion(f32[2048,2048]{1,0:T(8,128)} %fusion.133, bf16[1024,1024]{1,0:T(8,128)(2,1)} %collective-permute-done.11, bf16[1024,1024]{1,0:T(8,128)(2,1)} %get-tuple-element.100), kind=kOutput, calls=%fused_computation.144 | convolution fusion | flops 8638169088 | bytes 25165824 | tf_op jit(solution)/shard_map/dot_general | solution.py:35
  307.2 21.7 %all-to-all-done.5 = bf16[8,256,1024]{2,1,0:T(8,128)(2,1)} async-done(((bf16[8,256,1024]{2,1,0:T(8,128)(2,1)}), bf16[8,256,1024]{2,1,0:T(8,128)(2,1)}, u32[]{:S(2)}, u32[]{:S(2)}) %all-to-all-start.5) | async-done | bytes 4194336 | tf_op jit(solution)/shard_map/all_to_all | solution.py:44
  335.7 15.3 %fusion.137 = f32[2048,2048]{1,0:T(8,128)} fusion(bf16[1024,2048]{0,1:T(8,128)(2,1)} %bitcast.600, bf16[1024,1024]{1,0:T(8,128)(2,1)} %collective-permute-done, bf16[1024,1024]{1,0:T(8,128)(2,1)} %get-tuple-element.75), kind=kOutput, calls=%fused_computation.158 | convolution fusion | flops 8598323200 | bytes 25165824 | tf_op jit(solution)/shard_map/dot_general | solution.py:35
  351.0 16.4 %fusion.123 = bf16[2048,1024]{1,0:T(8,128)(2,1)} fusion(f32[2048,2048]{1,0:T(8,128)} %fusion.137, bf16[1024,1024]{1,0:T(8,128)(2,1)} %collective-permute-done.4, bf16[1024,1024]{1,0:T(8,128)(2,1)S(1)} %get-tuple-element.99), kind=kOutput, calls=%fused_computation.146 | convolution fusion | flops 8638169088 | bytes 25165824 | tf_op jit(solution)/shard_map/dot_general | solution.py:35
  367.4 21.4 %all-to-all-done.6 = bf16[8,256,1024]{2,1,0:T(8,128)(2,1)} async-done(((bf16[8,256,1024]{2,1,0:T(8,128)(2,1)}), bf16[8,256,1024]{2,1,0:T(8,128)(2,1)}, u32[]{:S(2)}, u32[]{:S(2)}) %all-to-all-start.6) | async-done | bytes 4194336 | tf_op jit(solution)/shard_map/all_to_all | solution.py:44
  419.2 28.8 %all-to-all-done.4 = bf16[8,256,1024]{2,1,0:T(8,128)(2,1)} async-done(((bf16[8,256,1024]{2,1,0:T(8,128)(2,1)}), bf16[8,256,1024]{2,1,0:T(8,128)(2,1)}, u32[]{:S(2)}, u32[]{:S(2)}) %all-to-all-start.4) | async-done | bytes 4194336 | tf_op jit(solution)/shard_map/all_to_all | solution.py:44
  454.1 22.8 %fusion.342 = bf16[2048,2048]{1,0:T(8,128)(2,1)S(1)} fusion(f32[2048,2048]{1,0:T(8,128)} %fusion.133, bf16[2048,1024]{1,0:T(8,128)(2,1)} %bitcast.606, bf16[1024,1024]{1,0:T(8,128)(2,1)} %collective-permute-done.11, bf16[1024,1024]{1,0:T(8,128)(2,1)} %get-tuple-element.100), kind=kOutput, calls=%fused_computation.39.clone.clone.clone.clone | convolution fusion | flops 8682209280 | bytes 33554432 | tf_op jit(solution)/shard_map/dot_general | solution.py:35
  549.0 29.4 %all-to-all-done.2 = bf16[8,128,2048]{2,1,0:T(8,128)(2,1)} async-done(((bf16[8,128,2048]{2,1,0:T(8,128)(2,1)}), bf16[8,128,2048]{2,1,0:T(8,128)(2,1)}, u32[]{:S(2)}, u32[]{:S(2)}) %all-to-all-start.2) | async-done | bytes 4194336 | tf_op jit(solution)/shard_map/all_to_all | solution.py:44
  615.2 24.6 %fusion.339 = bf16[2048,2048]{1,0:T(8,128)(2,1)} fusion(f32[2048,2048]{1,0:T(8,128)} %fusion.137, bf16[2048,1024]{1,0:T(8,128)(2,1)} %bitcast.615, bf16[1024,1024]{1,0:T(8,128)(2,1)} %collective-permute-done.4, bf16[1024,1024]{1,0:T(8,128)(2,1)S(1)} %copy-done.58), kind=kOutput, calls=%fused_computation.25.clone.clone.clone.clone.2 | convolution fusion | flops 8682209280 | bytes 33554432 | tf_op jit(solution)/shard_map/dot_general | solution.py:35
  654.4 25.8 %all-to-all-done.1 = bf16[8,128,2048]{2,1,0:T(8,128)(2,1)} async-done(((bf16[8,128,2048]{2,1,0:T(8,128)(2,1)}), bf16[8,128,2048]{2,1,0:T(8,128)(2,1)}, u32[]{:S(2)}, u32[]{:S(2)}) %all-to-all-start.1) | async-done | bytes 4194336 | tf_op jit(solution)/shard_map/all_to_all | solution.py:44
  713.4 35.7 %all-to-all-done = bf16[8,128,2048]{2,1,0:T(8,128)(2,1)} async-done(((bf16[8,128,2048]{2,1,0:T(8,128)(2,1)}), bf16[8,128,2048]{2,1,0:T(8,128)(2,1)}, u32[]{:S(2)}, u32[]{:S(2)}) %all-to-all-start) | async-done | bytes 4194336 | tf_op jit(solution)/shard_map/all_to_all | solution.py:44
  762.5 16.9 %fusion.120 = bf16[2048,1024]{1,0:T(8,128)(2,1)} fusion(f32[2048,2048]{1,0:T(8,128)} %fusion.131, bf16[1024,1024]{1,0:T(8,128)(2,1)} %collective-permute-done.8, bf16[1024,1024]{1,0:T(8,128)(2,1)} %get-tuple-element.102), kind=kOutput, calls=%fused_computation.143 | convolution fusion | flops 8638169088 | bytes 25165824 | tf_op jit(solution)/shard_map/dot_general | solution.py:35
  791.1 61.3 %all-to-all-done.7 = bf16[8,256,1024]{2,1,0:T(8,128)(2,1)} async-done(((bf16[8,256,1024]{2,1,0:T(8,128)(2,1)}), bf16[8,256,1024]{2,1,0:T(8,128)(2,1)}, u32[]{:S(2)}, u32[]{:S(2)}) %all-to-all-start.7) | async-done | bytes 4194336 | tf_op jit(solution)/shard_map/all_to_all | solution.py:44
  859.7 24.4 %fusion.68 = f32[2048,1024]{1,0:T(8,128)} fusion(bf16[2048,1024]{1,0:T(8,128)(2,1)} %all-gather.19.cloned.1.call-done, bf16[1024,2048]{1,0:T(8,128)(2,1)} %all-gather.17.cloned.1.call-done, bf16[1024,1024]{1,0:T(8,128)(2,1)} %collective-permute-done.20, bf16[1024,1024]{1,0:T(8,128)(2,1)} %get-tuple-element.82), kind=kOutput, calls=%fused_computation.90 | convolution fusion | flops 17226006528 | bytes 20971520 | tf_op jit(solution)/shard_map/dot_general | solution.py:35
  888.9 24.7 %fusion.76 = f32[2048,1024]{1,0:T(8,128)} fusion(bf16[2048,1024]{1,0:T(8,128)(2,1)} %all-gather.11.cloned.1.call-done, bf16[1024,2048]{1,0:T(8,128)(2,1)} %all-gather.9.cloned.1.call-done, bf16[1024,1024]{1,0:T(8,128)(2,1)} %collective-permute-done.14, bf16[1024,1024]{1,0:T(8,128)(2,1)} %get-tuple-element.81), kind=kOutput, calls=%fused_computation.94 | convolution fusion | flops 17226006528 | bytes 20971520 | tf_op jit(solution)/shard_map/dot_general | solution.py:35
  967.5 24.6 %fusion.72 = f32[2048,1024]{1,0:T(8,128)} fusion(bf16[2048,1024]{1,0:T(8,128)(2,1)} %all-gather.15.cloned.1.call-done, bf16[1024,2048]{1,0:T(8,128)(2,1)} %all-gather.13.cloned.1.call-done, bf16[1024,1024]{1,0:T(8,128)(2,1)} %collective-permute-done.17, bf16[1024,1024]{1,0:T(8,128)(2,1)} %get-tuple-element.79), kind=kOutput, calls=%fused_computation.92 | convolution fusion | flops 17226006528 | bytes 20971520 | tf_op jit(solution)/shard_map/dot_general | solution.py:35
  1010.9 49.1 %all-gather.21.cloned.1.call-done = bf16[1024,2048]{1,0:T(8,128)(2,1)} async-done(((bf16[128,2048]{1,0:T(8,128)(2,1)}), bf16[1024,2048]{1,0:T(8,128)(2,1)}) %all-gather.21.cloned.1.call-update) | async-done | bytes 4194320 | tf_op jit(solution)/shard_map/all_gather | solution.py:112
  1060.0 24.3 %fusion.64 = f32[2048,1024]{1,0:T(8,128)} fusion(bf16[2048,1024]{1,0:T(8,128)(2,1)} %all-gather.23.cloned.1.call-done, bf16[1024,2048]{1,0:T(8,128)(2,1)} %all-gather.21.cloned.1.call-done, bf16[1024,1024]{1,0:T(8,128)(2,1)} %collective-permute-done.23, bf16[1024,1024]{1,0:T(8,128)(2,1)S(1)} %get-tuple-element.80), kind=kOutput, calls=%fused_computation.88 | convolution fusion | flops 17226006528 | bytes 20971520 | tf_op jit(solution)/shard_map/dot_general | solution.py:35
  (363 shorter events, 501.2 us)
Async XLA Ops:
  13.7 85.8 %collective-permute-start.2 = (bf16[1024,1024]{1,0:T(8,128)(2,1)}, bf16[1024,1024]{1,0:T(8,128)(2,1)}, u32[]{:S(2)}, u32[]{:S(2)}) collective-permute-start(bf16[1024,1024]{1,0:T(8,128)(2,1)} %get-tuple-element.76), channel_id=1, source_target_pairs={{0,1},{1,0},{2,3},{3,2},{4,5},{5,4},{6,7},{7,6},{8,9},{9,8},{10,11... | collective-permute-start | bytes 6291464 | tf_op jit(solution)/shard_map/ppermute | solution.py:31
  16.5 98.2 %collective-permute-start.1 = (bf16[1024,1024]{1,0:T(8,128)(2,1)S(1)}, bf16[1024,1024]{1,0:T(8,128)(2,1)}, u32[]{:S(2)}, u32[]{:S(2)}) collective-permute-start(bf16[1024,1024]{1,0:T(8,128)(2,1)S(1)} %get-tuple-element.101), channel_id=1, source_target_pairs={{0,1},{1,0},{2,3},{3,2},{4,5},{5,4},{6,7},{7,6},{8,9},{9,8},{10,11... | collective-permute-start | bytes 6291464 | tf_op jit(solution)/shard_map/ppermute | solution.py:31
  17.2 138.1 %collective-permute-start.9 = (bf16[1024,1024]{1,0:T(8,128)(2,1)}, bf16[1024,1024]{1,0:T(8,128)(2,1)}, u32[]{:S(2)}, u32[]{:S(2)}) collective-permute-start(bf16[1024,1024]{1,0:T(8,128)(2,1)} %get-tuple-element.77), channel_id=1, source_target_pairs={{0,1},{1,0},{2,3},{3,2},{4,5},{5,4},{6,7},{7,6},{8,9},{9,8},{10,11... | collective-permute-start | bytes 6291464 | tf_op jit(solution)/shard_map/ppermute | solution.py:31
  17.2 152.1 %collective-permute-start.8 = (bf16[1024,1024]{1,0:T(8,128)(2,1)}, bf16[1024,1024]{1,0:T(8,128)(2,1)}, u32[]{:S(2)}, u32[]{:S(2)}) collective-permute-start(bf16[1024,1024]{1,0:T(8,128)(2,1)} %get-tuple-element.102), channel_id=1, source_target_pairs={{0,1},{1,0},{2,3},{3,2},{4,5},{5,4},{6,7},{7,6},{8,9},{9,8},{10,11... | collective-permute-start | bytes 6291464 | tf_op jit(solution)/shard_map/ppermute | solution.py:31
  155.1 86.8 %collective-permute-start.3 = (f32[1024,1024]{1,0:T(8,128)}, f32[1024,1024]{1,0:T(8,128)}, u32[]{:S(2)}, u32[]{:S(2)}) collective-permute-start(f32[1024,1024]{1,0:T(8,128)} %slice.241), channel_id=1, source_target_pairs={{0,1},{1,0},{2,3},{3,2},{4,5},{5,4},{6,7},{7,6},{8,9},{9,8},{10,11... | collective-permute-start | bytes 12582920 | tf_op jit(solution)/shard_map/ppermute | solution.py:31
  208.7 126.9 %collective-permute-start = (bf16[1024,1024]{1,0:T(8,128)(2,1)}, bf16[1024,1024]{1,0:T(8,128)(2,1)}, u32[]{:S(2)}, u32[]{:S(2)}) collective-permute-start(bf16[1024,1024]{1,0:T(8,128)(2,1)} %get-tuple-element.75), channel_id=1, source_target_pairs={{0,1},{1,0},{2,3},{3,2},{4,5},{5,4},{6,7},{7,6},{8,9},{9,8},{10,11... | collective-permute-start | bytes 6291464 | tf_op jit(solution)/shard_map/ppermute | solution.py:31
  208.9 66.1 %collective-permute-start.7 = (bf16[1024,1024]{1,0:T(8,128)(2,1)}, bf16[1024,1024]{1,0:T(8,128)(2,1)}, u32[]{:S(2)}, u32[]{:S(2)}) collective-permute-start(bf16[1024,1024]{1,0:T(8,128)(2,1)} %get-tuple-element.78), channel_id=1, source_target_pairs={{0,1},{1,0},{2,3},{3,2},{4,5},{5,4},{6,7},{7,6},{8,9},{9,8},{10,11... | collective-permute-start | bytes 6291464 | tf_op jit(solution)/shard_map/ppermute | solution.py:31
  290.3 60.7 %collective-permute-start.4 = (bf16[1024,1024]{1,0:T(8,128)(2,1)S(1)}, bf16[1024,1024]{1,0:T(8,128)(2,1)}, u32[]{:S(2)}, u32[]{:S(2)}) collective-permute-start(bf16[1024,1024]{1,0:T(8,128)(2,1)S(1)} %get-tuple-element.99), channel_id=1, source_target_pairs={{0,1},{1,0},{2,3},{3,2},{4,5},{5,4},{6,7},{7,6},{8,9},{9,8},{10,11... | collective-permute-start | bytes 6291464 | tf_op jit(solution)/shard_map/ppermute | solution.py:31
  454.1 405.6 %all-gather.19.cloned.1.call-start = ((), (), s32[]{:S(2)}) async-start(), calls=%async_computation.13 | async-start | bytes 4718592 | tf_op jit(solution)/shard_map/all_gather | solution.py:106
  507.2 71.1 %all-to-all-start.2 = ((bf16[8,128,2048]{2,1,0:T(8,128)(2,1)}), bf16[8,128,2048]{2,1,0:T(8,128)(2,1)}, u32[]{:S(2)}, u32[]{:S(2)}) async-start(bf16[8,128,2048]{2,1,0:T(8,128)(2,1)} %bitcast.599), calls=%async_computation.2 | async-start | bytes 8388608 | tf_op jit(solution)/shard_map/all_to_all | solution.py:44
  513.3 346.4 %all-gather.17.cloned.1.call-start = ((), (), s32[]{:S(2)}) async-start(), calls=%async_computation.12 | async-start | bytes 4718592 | tf_op jit(solution)/shard_map/all_gather | solution.py:112
  608.4 71.8 %all-to-all-start.1 = ((bf16[8,128,2048]{2,1,0:T(8,128)(2,1)}), bf16[8,128,2048]{2,1,0:T(8,128)(2,1)}, u32[]{:S(2)}, u32[]{:S(2)}) async-start(bf16[8,128,2048]{2,1,0:T(8,128)(2,1)} %bitcast.607), calls=%async_computation.1 | async-start | bytes 8388608 | tf_op jit(solution)/shard_map/all_to_all | solution.py:44
  615.0 273.9 %all-gather.11.cloned.1.call-start = ((), (), s32[]{:S(2)}) async-start(), calls=%async_computation.9 | async-start | bytes 4718592 | tf_op jit(solution)/shard_map/all_gather | solution.py:106
  680.2 68.9 %all-to-all-start = ((bf16[8,128,2048]{2,1,0:T(8,128)(2,1)}), bf16[8,128,2048]{2,1,0:T(8,128)(2,1)}, u32[]{:S(2)}, u32[]{:S(2)}) async-start(bf16[8,128,2048]{2,1,0:T(8,128)(2,1)} %bitcast.601), calls=%async_computation | async-start | bytes 8388608 | tf_op jit(solution)/shard_map/all_to_all | solution.py:44
  687.8 201.1 %all-gather.9.cloned.1.call-start = ((), (), s32[]{:S(2)}) async-start(), calls=%async_computation.8 | async-start | bytes 4718592 | tf_op jit(solution)/shard_map/all_gather | solution.py:112
  759.3 208.1 %all-gather.15.cloned.1.call-start = ((), (), s32[]{:S(2)}) async-start(), calls=%async_computation.11 | async-start | bytes 4718592 | tf_op jit(solution)/shard_map/all_gather | solution.py:106
  759.9 207.6 %all-gather.13.cloned.1.call-start = ((), (), s32[]{:S(2)}) async-start(), calls=%async_computation.10 | async-start | bytes 4718592 | tf_op jit(solution)/shard_map/all_gather | solution.py:112
  779.4 73.0 %all-to-all-start.7 = ((bf16[8,256,1024]{2,1,0:T(8,128)(2,1)}), bf16[8,256,1024]{2,1,0:T(8,128)(2,1)}, u32[]{:S(2)}, u32[]{:S(2)}) async-start(bf16[8,256,1024]{2,1,0:T(8,128)(2,1)} %bitcast.613), calls=%async_computation.7 | async-start | bytes 8388608 | tf_op jit(solution)/shard_map/all_to_all | solution.py:44
  785.8 225.1 %all-gather.23.cloned.1.call-start = ((), (), s32[]{:S(2)}) async-start(), calls=%async_computation.15 | async-start | bytes 4718592 | tf_op jit(solution)/shard_map/all_gather | solution.py:106
  790.6 69.1 %collective-permute-start.20 = (bf16[1024,1024]{1,0:T(8,128)(2,1)}, bf16[1024,1024]{1,0:T(8,128)(2,1)}, u32[]{:S(2)}, u32[]{:S(2)}) collective-permute-start(bf16[1024,1024]{1,0:T(8,128)(2,1)} %get-tuple-element.82), channel_id=1, source_target_pairs={{0,1},{1,0},{2,3},{3,2},{4,5},{5,4},{6,7},{7,6},{8,9},{9,8},{10,11... | collective-permute-start | bytes 6291464 | tf_op jit(solution)/shard_map/ppermute | solution.py:31
  790.7 98.2 %collective-permute-start.14 = (bf16[1024,1024]{1,0:T(8,128)(2,1)}, bf16[1024,1024]{1,0:T(8,128)(2,1)}, u32[]{:S(2)}, u32[]{:S(2)}) collective-permute-start(bf16[1024,1024]{1,0:T(8,128)(2,1)} %get-tuple-element.81), channel_id=1, source_target_pairs={{0,1},{1,0},{2,3},{3,2},{4,5},{5,4},{6,7},{7,6},{8,9},{9,8},{10,11... | collective-permute-start | bytes 6291464 | tf_op jit(solution)/shard_map/ppermute | solution.py:31
  859.5 200.6 %all-gather.21.cloned.1.call-start = ((), (), s32[]{:S(2)}) async-start(), calls=%async_computation.14 | async-start | bytes 4718592 | tf_op jit(solution)/shard_map/all_gather | solution.py:112
  967.0 93.0 %collective-permute-start.23 = (bf16[1024,1024]{1,0:T(8,128)(2,1)S(1)}, bf16[1024,1024]{1,0:T(8,128)(2,1)}, u32[]{:S(2)}, u32[]{:S(2)}) collective-permute-start(bf16[1024,1024]{1,0:T(8,128)(2,1)S(1)} %get-tuple-element.80), channel_id=1, source_target_pairs={{0,1},{1,0},{2,3},{3,2},{4,5},{5,4},{6,7},{7,6},{8,9},{9,8},{10,11... | collective-permute-start | bytes 6291464 | tf_op jit(solution)/shard_map/ppermute | solution.py:31
  996.8 107.1 %collective-permute-start.19 = (f32[1024,1024]{1,0:T(8,128)}, f32[1024,1024]{1,0:T(8,128)}, u32[]{:S(2)}, u32[]{:S(2)}) collective-permute-start(f32[1024,1024]{1,0:T(8,128)} %slice.247), channel_id=1, source_target_pairs={{0,1},{1,0},{2,3},{3,2},{4,5},{5,4},{6,7},{7,6},{8,9},{9,8},{10,11... | collective-permute-start | bytes 12582920 | tf_op jit(solution)/shard_map/ppermute | solution.py:31
  (89 other events, 1255.4 us)
Sparse Core Ops, SparseCore 0:
  500.0 89.0 all-gather.18
  591.3 92.1 all-gather.16
  685.7 85.0 all-gather.10
  773.4 89.4 all-gather.8
  864.9 47.7 all-gather.14
  914.8 46.9 all-gather.12
  963.9 46.9 all-gather.22
  1013.0 46.9 all-gather.20

commit v2 on v0

v2 whole, which is shorter than its diff:
```python
import jax
import jax.numpy as jnp
from jax import lax
from jax.experimental import pallas as pl
from jax.experimental.pallas import tpu as pltpu
from jax.sharding import PartitionSpec as P

LEARN_RATE = 0.005
BETA_ONE = 0.9
BETA_TWO = 0.95
ADAM_EPS = 1e-8
WEIGHT_DECAY = 0.1
MICROBATCHES = 2
ADAM_STEP = 2
F32 = jnp.float32
BF16 = jnp.bfloat16
MESH = pl.DeviceIdType.MESH
GELU_C = 0.7978845608028654
GELU_K = 0.044715
AXES = 'zyx'
ORDERS = ('xyz', 'yzx', 'zxy')
COLS = {'d': ((0, 384), (384, 384), (768, 256)), 'u': ((0, 640), (640, 640), (1280, 768))}
ROWS = {'d': 256, 'u': 128}
WIDE = {'d': 1024, 'u': 2048}
T = 1024
D = 1024
H = 2048
TM = 256
TF = 512
PAIR = (0, 1)
QUADS = 4
SEMS = 230
CHIPS = 8
SUB = 16
STEPS = {'d': (1, 2, 3, 6, 7), 'u': (1, 2, 3, 4, 5, 6, 7)}
MATS = {'A': (0, 1, 'd'), 'B': (0, 1, 'u'), 'C': (0, 0, 'd'), 'D': (0, 0, 'u'), 'E': (1, 1, 'd'), 'F': (1, 1, 'u'), 'G': (1, 0, 'd'), 'H': (1, 0, 'u')}
ORDER = ('jjjjjjAjjjAjBjjjjABCjjDAjjCjEjDjjCDjFDjDBHFCEDHFBD', 'FGHBCHHFBGjjHjBAjGjjFEGHjjGjEjFjjjjEjjjjjj',)

def adam_update(acc_part, grad_new, master, moment_one, moment_two):
    grad_mean = (acc_part + grad_new) / MICROBATCHES
    moment_one = BETA_ONE * moment_one + (1.0 - BETA_ONE) * grad_mean
    moment_two = BETA_TWO * moment_two + (1.0 - BETA_TWO) * grad_mean * grad_mean
    corr_one = 1.0 - BETA_ONE ** ADAM_STEP
    corr_two = 1.0 - BETA_TWO ** ADAM_STEP
    step_dir = (moment_one / corr_one) / (jnp.sqrt(moment_two / corr_two) + ADAM_EPS)
    master = master - LEARN_RATE * (step_dir + WEIGHT_DECAY * master)
    return master, moment_one, moment_two


def jobs_of():
    for s in PAIR:
        for l in reversed(PAIR):
            for g in range(QUADS // (1 if (s, l) == (0, 1) else 2)):
                yield 'k', s, l, g
            if l:
                yield 'bk', s, l, 1
                yield 'bk', s, l, 0
            yield 'j3', s, l, 0
            if l:
                yield 'cb', s, l, 0
            yield 'j3', s, l, 1
    for s in PAIR:
        for l in PAIR:
            for name, half in (('f1', 1 - l), ('f1', l), ('f2', 1), ('f2', 0), ('cf', 0)):
                yield name, s, l, half


def gelu_parts(h):
    sq = h * h
    th = jnp.tanh(GELU_C * (h + GELU_K * (h * sq)))
    return sq, th


def dot(a, b, ca, cb):
    return lax.dot_general(a, b, (((ca,), (cb,)), ((), ())), preferred_element_type=F32)


def step_kernel(*refs):
    it = iter(refs)
    take = lambda n: [next(it) for i in range(n)]
    x_saved, grad_out, x_next, w_up, w_down = take(5)
    acc, mast, mom1, mom2 = [dict(zip('ud', take(2))) for i in range(4)]
    nmast, nmom1, nmom2 = [dict(zip('ud', take(2))) for i in range(3)]
    (y_out,) = take(1)
    xr, tokr, pr = take(3)
    part, r1, r2o, r2f, r3, aw = [dict(zip('du', take(2))) for i in range(6)]
    gd, go, gx, ws = take(4)
    xv, yv, w1v, w2v, av, hv, fst, dwd, dwu = take(9)
    sb, so, r3v = [dict(zip('du', take(2))) for i in range(3)]
    ssem, rsem, w1sem, w2sem, xsem, ysem, dwsem, sbsem, msem = take(9)

    me = lax.axis_index('fsdp')
    pos = {'z': lax.div(me, 8), 'y': lax.rem(lax.div(me, 4), 2), 'x': lax.rem(lax.div(me, 2), 2)}
    core = lax.rem(me, 2)
    flip = {a: 1 - pos[a] for a in AXES}
    peer = {a: me + step * (1 - 2 * pos[a]) for a, step in (('z', 8), ('y', 4), ('x', 2))}
    peer['core'] = me + 1 - 2 * core
    spot = tuple(pos[a] for a in AXES)

    sem_ids = {}
    sends = {}

    def remote(key, src, dst, axis):
        n = sem_ids.setdefault(key, len(sem_ids))
        cp = pltpu.make_async_remote_copy(src_ref=src, dst_ref=dst, send_sem=ssem.at[n], recv_sem=rsem.at[n], device_id=(peer[axis],), device_id_type=MESH)
        cp.start()
        sends[key] = cp

    recv = lambda key: sends[key].wait_recv()
    unsent = set()

    def wait_send(key):
        if key in sends and key not in unsent:
            unsent.add(key)
            sends[key].wait_send()

    def cut(ref, i, fix, c0, n):
        return ref.at[(i,) + tuple(fix.get(a, slice(None)) for a in AXES) + (slice(None), pl.ds(c0, n))]

    def local(src, dst, sem):
        cp = pltpu.make_async_copy(src, dst, sem)
        cp.start()
        return cp

    loads = {'w1': [], 'w2': [], 'xa': [], 'xb': [], 'ya': [], 'yb': []}

    def ready(*names):
        for name in names:
            for cp in loads[name]:
                cp.wait()
            loads[name] = []

    def load_w1(s, l):
        loads['w1'] = [local(w_up.at[s, l, :, pl.ds(512 * c + 256 * core, 256)], w1v.at[:, pl.ds(256 * c, 256)], w1sem.at[c]) for c in range(8)]

    def load_w2(s, l):
        loads['w2'] = [local(w_down.at[s, l, c, core], w2v.at[pl.ds(256 * c, 256)], w2sem.at[c]) for c in range(8)]

    def load_new(kind, i):
        dst, sem, name, rows = (w1v, w1sem, 'w1', 128) if kind == 'u' else (w2v, w2sem, 'w2', 256)
        loads[name] = [local(aw[kind].at[i, c // 4, (c // 2) % 2, c % 2], dst.at[pl.ds(rows * c, rows)], sem.at[c]) for c in range(8)]

    def load_x(half, src):
        loads[('xa', 'xb')[half]] = [local(src, xv.at[pl.ds(T * half, T)], xsem.at[half])]

    def load_y(half, src):
        loads[('ya', 'yb')[half]] = [local(src, yv.at[pl.ds(T * half, T)], ysem.at[half])]

    def slab(n, size):
        return pl.ds(pl.multiple_of(n * size, size), size)

    def quad(g):
        return lax.rem(pos['z'] + 1 + lax.div(g, 2), 2), lax.rem(pos['y'] + 1 + lax.rem(g, 2), 2)

    def backward(i, g0, count, hook=None):
        def block(g, hook=None):
            zz, yy = quad(g)
            fs = slab(2 * zz + yy, TF)

            def body(n, carry):
                ts = slab(n, TM)
                h = dot(xv[ts, :], w1v[:, fs], 1, 0)
                da = dot(yv[ts, :], w2v[fs, :], 1, 1)
                sq, th = gelu_parts(h)
                cdf = 0.5 * (1.0 + th)
                av[ts, fs] = (h * cdf).astype(BF16)
                slope = cdf + 0.5 * h * (1.0 - th * th) * (GELU_C * (1.0 + 3.0 * GELU_K * sq))
                hv[ts, fs] = (da * slope).astype(BF16)
                return carry
            tiles = T // TM
            if hook is not None:
                lax.fori_loop(0, tiles, body, 0)
                hook()
                lax.fori_loop(tiles, 2 * tiles, body, 0)
            else:
                lax.fori_loop(0, 2 * tiles, body, 0)

            def out(n):
                return pltpu.make_async_copy(dwd.at[n], part['d'].at[i, zz, yy, n], dwsem.at[n])

            def body2(n, carry):
                f0 = slab(2 * (2 * zz + yy) + n, TM)

                def inner(c, carry):
                    cs = slab(c, TF)
                    dwd[n, :, cs] = dot(av[:, f0], yv[:, cs], 0, 0).astype(BF16)
                    return carry
                lax.fori_loop(0, D // TF, inner, 0)
                out(n).start()
                return carry
            lax.fori_loop(0, 2, body2, 0)
            for n in PAIR:
                out(n).wait()
        if count == 1:
            block(jnp.int32(g0), hook)
        else:
            def each(g, carry):
                block(g)
                return carry
            lax.fori_loop(g0, g0 + count, each, 0)

    def j3(i, half):
        def out(n):
            return pltpu.make_async_copy(dwu.at[n], part['u'].at[i, half, n], dwsem.at[n])

        def body(n, carry):
            def inner(c, carry):
                fs = slab(c, TF)
                res = dot(xv[:, slab(2 * half + n, TM)], hv[:, fs], 0, 0).astype(BF16)
                for e in PAIR:
                    dwu[n, e, :, fs] = res[128 * e:128 * e + 128]
                return carry
            lax.fori_loop(0, H // TF, inner, 0)
            out(n).start()
            return carry
        lax.fori_loop(0, 2, body, 0)
        for n in PAIR:
            out(n).wait()

    def proj(half, src, dst, w, cb, send=None):
        def body(n, carry):
            def inner(c, carry):
                cs = slab(c, TF)
                wt = w[cs, :] if cb else w[:, cs]
                fst[dst, slab(n, TM), cs] = dot(src[slab(T // TM * half + n, TM), :], wt, 1, cb)
                return carry
            return lax.fori_loop(0, D // TF, inner, carry)
        if send is None:
            lax.fori_loop(0, T // TM, body, 0)
            return
        for e in PAIR:
            lax.fori_loop(2 * e, 2 * e + 2, body, 0)
            rows = pl.ds(TF * e, TF)
            remote(('pr', send, e), fst.at[0, rows], pr.at[send, rows], 'core')

    def f1(half):
        def body(n, carry):
            ts = slab(T // TM * half + lax.div(n, H // TF), TM)
            fs = slab(lax.rem(n, H // TF), TF)
            h = dot(xv[ts, :], w1v[:, fs], 1, 0)
            sq, th = gelu_parts(h)
            av[ts, fs] = (h * (0.5 * (1.0 + th))).astype(BF16)
            return carry
        lax.fori_loop(0, (T // TM) * (H // TF), body, 0)

    def combine(n_pr, base):
        cps = []
        for e in PAIR:
            recv(('pr', n_pr, e))
            wait_send(('pr', n_pr, e))
            rows = pl.ds(TF * e, TF)
            cps.append(local(pr.at[n_pr, rows], fst.at[0, rows], msem.at[2 * e]))
        for e in PAIR:
            cps[e].wait()

            def body(n, carry):
                rows = slab(n, SUB)
                base[rows, :] = (base[rows, :].astype(F32) + (fst[1, rows, :] + fst[0, rows, :])).astype(BF16)
                return carry
            lax.fori_loop(TF * e // SUB, TF * (e + 1) // SUB, body, 0)

    def streams(kind):
        return zip(range(3), COLS[kind], ORDERS)

    last_so = {'d': None, 'u': None}
    last_gx = [None]
    first = {}

    def fetch(kind, items):
        cps = [local(src, dst, sbsem.at[n]) for n, (src, dst) in enumerate(items)]
        for cp in cps:
            cp.wait()

    def send_own(kind, m):
        i = 2 * m[0] + m[1]
        for q, (c0, n), (a, b, c) in streams(kind):
            fix = {a: pos[a], b: flip[b]}
            remote(('r2o', m, q), cut(part[kind], i, fix, c0, n), cut(r2o[kind], i, fix, c0, n), b)

    def send_half(kind, m, fix, which=AXES):
        i = 2 * m[0] + m[1]
        for q, (c0, n), (a, b, c) in streams(kind):
            if a in which:
                where = {**fix, a: flip[a]}
                key = ('r1', m, q)
                first.setdefault(key, []).append(key + (len(first.get(key, ())),))
                remote(first[key][-1], cut(part[kind], i, where, c0, n), cut(r1[kind], i, where, c0, n), a)

    def service(m, step):
        s, l, kind = m
        i = 2 * s + l
        rows, wide = ROWS[kind], WIDE[kind]
        pa, a1, a2, a3, a4 = part[kind], r1[kind], r2o[kind], r2f[kind], r3[kind]
        key = lambda name, q: (name, m, q)
        if step == 1:
            for q, (c0, n), (a, b, c) in streams(kind):
                for k in first[key('r1', q)]:
                    recv(k)
                fix = {a: pos[a], b: flip[b]}
                remote(key('r2f', q), cut(a1, i, fix, c0, n), cut(a3, i, fix, c0, n), b)
        if step == 2:
            items = []
            for q, (c0, n), (a, b, c) in streams(kind):
                recv(key('r2o', q))
                recv(key('r2f', q))
                fix = {a: pos[a], b: pos[b], c: flip[c]}
                for e, src in enumerate((pa, a1, a2, a3)):
                    items.append((cut(src, i, fix, c0, n), sb[kind].at[e, :, pl.ds(c0, n)]))
            if last_so[kind] is not None:
                for q in range(3):
                    wait_send(('r3', last_so[kind], q))
            last_so[kind] = m
            fetch(kind, items)

            def body(n, carry):
                r = slab(n, SUB)
                v = sb[kind]
                so[kind][r, :] = (v[0, r, :].astype(F32) + v[1, r, :].astype(F32)) + (v[2, r, :].astype(F32) + v[3, r, :].astype(F32))
                return carry
            lax.fori_loop(0, rows // SUB, body, 0)
            for q, (c0, n), (a, b, c) in streams(kind):
                remote(key('r3', q), so[kind].at[:, pl.ds(c0, n)], a4.at[i, :, pl.ds(c0, n)], c)
        if step == 3:
            for q in range(3):
                recv(key('r3', q))
            if kind == 'u' and last_gx[0] is not None:
                wait_send(last_gx[0])
            items = [(src.at[(i,) + spot], sb[kind].at[e]) for e, src in enumerate((pa, a1, a2, a3))]
            fetch(kind, items + [(a4.at[i], r3v[kind])])

            def body(n, carry):
                r = slab(n, SUB)
                v = sb[kind]
                r3v[kind][r, :] = (v[0, r, :].astype(F32) + v[1, r, :].astype(F32)) + (v[2, r, :].astype(F32) + v[3, r, :].astype(F32)) + r3v[kind][r, :]
                return carry
            lax.fori_loop(0, rows // SUB, body, 0)
            if kind == 'd':
                local(r3v[kind], gd.at[i], msem.at[1]).wait()
                spec = pl.BlockSpec((64, D), lambda j: (j, 0))

                def body_d(g, ac, ma, m1, m2, oma, om1, om2, ow):
                    oma[...], om1[...], om2[...] = adam_update(ac[...], g[...], ma[...], m1[...], m2[...])
                    ow[...] = oma[...].astype(BF16)
                pltpu.emit_pipeline(body_d, grid=(4,), in_specs=[spec] * 5, out_specs=[spec] * 4)(
                    gd.at[i], acc['d'].at[s, l], mast['d'].at[s, l], mom1['d'].at[s, l], mom2['d'].at[s, l],
                    nmast['d'].at[s, l], nmom1['d'].at[s, l], nmom2['d'].at[s, l], aw['d'].at[(i,) + spot])
            else:
                last_gx[0] = ('gx', m)
                remote(('gx', m), r3v[kind].at[pl.ds(pl.multiple_of(64 * (1 - core), 64), 64)], gx.at[i], 'core')
                local(r3v[kind].at[pl.ds(pl.multiple_of(64 * core, 64), 64)], go.at[i], msem.at[1]).wait()
        if step == 4:
            recv(('gx', m))
            spec = pl.BlockSpec((64, 512), lambda j: (0, j))
            part_spec = pl.BlockSpec((64, 256), lambda j: (0, j))
            own_spec = pl.BlockSpec((64, 256), lambda j: (core, j))

            def body_u(g0, g1, ac, ma, m1, m2, oma, om1, om2, ow0, ow1):
                low = jnp.where(core == 0, g0[...], g1[...])
                high = jnp.where(core == 0, g1[...], g0[...])
                for h, g in ((0, low), (1, high)):
                    c = slice(256 * h, 256 * h + 256)
                    oma[:, c], om1[:, c], om2[:, c] = adam_update(ac[:, c], g, ma[:, c], m1[:, c], m2[:, c])
                wl, wh = oma[:, :256], oma[:, 256:]
                ow0[...] = jnp.where(core == 0, wl, wh).astype(BF16)
                ow1[...] = jnp.where(core == 0, wh, wl).astype(BF16)
            pltpu.emit_pipeline(body_u, grid=(8,), in_specs=[part_spec] * 2 + [spec] * 4, out_specs=[spec] * 3 + [own_spec, part_spec])(
                go.at[i], gx.at[i], acc['u'].at[s, l], mast['u'].at[s, l], mom1['u'].at[s, l], mom2['u'].at[s, l],
                nmast['u'].at[s, l], nmom1['u'].at[s, l], nmom2['u'].at[s, l], aw['u'].at[(i,) + spot], ws.at[i])
            remote(('ws', m), ws.at[i], aw['u'].at[(i,) + spot + (pl.ds(pl.multiple_of(64 * core, 64), 64),)], 'core')
        if step == 5:
            recv(('ws', m))
        w = aw[kind]
        if (kind == 'd' and step == 3) or step == 5:
            for q, (c0, n), (a, b, c) in streams(kind):
                v = cut(w, i, pos, c0, n)
                remote(key('a1', q), v, v, c)
        if step == 6:
            for q, (c0, n), (a, b, c) in streams(kind):
                recv(key('a1', q))
                v = cut(w, i, {a: pos[a], b: pos[b]}, c0, n)
                remote(key('a2', q), v, v, b)
        if step == 7:
            for q, (c0, n), (a, b, c) in streams(kind):
                recv(key('a2', q))
                v = cut(w, i, {a: pos[a]}, c0, n)
                remote(key('a3', q), v, v, a)

    load_x(0, x_saved.at[0, 1, 0])
    load_w1(0, 1)
    load_y(0, grad_out.at[0, 0])
    load_w2(0, 1)
    barrier = pltpu.get_barrier_semaphore()
    for axis in ('x', 'y', 'z', 'core'):
        pl.semaphore_signal(barrier, inc=1, device_id=(peer[axis],), device_id_type=MESH)
    pl.semaphore_wait(barrier, 4)
    toks = [x_saved.at[0, 1, 0], grad_out.at[0, 0], x_saved.at[0, 0, 0], x_saved.at[1, 1, 0], grad_out.at[1, 0], x_saved.at[1, 0, 0], x_next.at[0, 0], x_next.at[1, 0]]
    xid = {(0, 1): 0, (0, 0): 2, (1, 1): 3, (1, 0): 5}
    for n, src in enumerate(toks):
        remote(('tok', n), src, xr.at[n], 'core')

    following = {(0, 1): (0, 0), (0, 0): (1, 1), (1, 1): (1, 0), (1, 0): None}
    jobs = jobs_of()
    steps = {m: iter(STEPS[m[2]]) for m in MATS.values()}
    for token in ''.join(ORDER):
        if token in MATS:
            service(MATS[token], next(steps[MATS[token]]))
            continue
        name, s, l, half = next(jobs)
        i = 2 * s + l
        nxt = following[s, l]
        own = pl.ds(0, T)
        if name == 'k':
            def arrive():
                recv(('tok', 0))
                load_x(1, xr.at[0])
                recv(('tok', 1))
                load_y(1, xr.at[1])
                ready('xb', 'yb')
            m = (s, l, 'd')
            start = (s, l) == (0, 1)
            if half == 0:
                ready('xa', 'ya', 'w1', 'w2')
                if l == 0:
                    recv(('tk', s))
                    load_y(1, tokr.at[s])
                if not start:
                    ready('xb', 'yb')
            g = half if start else 2 * half
            backward(i, g, 1 if start else 2, arrive if start and half == 0 else None)
            zz, yy = quad(jnp.int32(g))
            g += 0 if start else 1
            send_half('d', m, {'z': zz, 'y': yy} if start else {'z': zz}, 'x')
            if g == 1:
                send_half('d', m, {}, 'z')
            if g == (2 if start else QUADS - 1):
                send_half('d', m, {}, 'y')
            if g == QUADS - 1:
                send_own('d', m)
                if nxt:
                    load_w2(*nxt)
                if l == 0 and nxt:
                    load_w1(*nxt)
                    wait_send(('tk', s))
                    load_y(0, grad_out.at[nxt[0], 0])
                    recv(('tok', 4))
                    load_y(1, xr.at[4])
        elif name == 'bk':
            proj(half, hv, 1 - half, w1v, 1, s if half else None)
            if half == 0:
                load_w1(*nxt)
        elif name == 'j3':
            j3(i, half)
            if half:
                send_half('u', (s, l, 'u'), {})
                send_own('u', (s, l, 'u'))
                n = xid[nxt] if nxt else 6
                load_x(0, x_saved.at[nxt[0], nxt[1], 0] if nxt else x_next.at[0, 0])
                recv(('tok', n))
                load_x(1, xr.at[n])
        elif name == 'cb':
            combine(s, yv)
            remote(('tk', s), yv.at[own], tokr.at[s], 'core')
        elif name == 'f1':
            if half == 1 - l:
                for q in range(3):
                    recv(('a3', (s, l, 'u'), q))
                load_new('u', i)
                if l == 0:
                    ready('xa', 'xb')
                ready('w1')
            elif l:
                recv(('tk', 2 + s))
                load_x(1, tokr.at[2 + s])
                ready('xb')
            f1(half)
        elif name == 'f2':
            if half:
                for q in range(3):
                    recv(('a3', (s, l, 'd'), q))
                load_new('d', i)
                ready('w2')
            proj(half, av, 1 - half, w2v, 0, 2 + i if half else None)
        elif name == 'cf':
            if l:
                wait_send(('tk', 2 + s))
            combine(2 + i, xv)
            if l == 0:
                remote(('tk', 2 + s), xv.at[own], tokr.at[2 + s], 'core')
            else:
                local(xv.at[own], y_out.at[s, 0], msem.at[2]).wait()
                if s == 0:
                    load_x(0, x_next.at[1, 0])
                    recv(('tok', 7))
                    load_x(1, xr.at[7])
    for key in sends:
        wait_send(key)


def solution(mesh):
    tok_spec = P(None, 'fsdp')
    layer_spec = P(None, None, 'fsdp')
    rep_spec = P()

    def device_step(x_saved, grad_out, x_next, w_up, w_down, *state):
        def sds(shape, dtype=F32):
            return jax.ShapeDtypeStruct(shape, dtype)
        up, down = (2, 2, 64, 4096), (2, 2, 256, 1024)
        cube = (4, 2, 2, 2)
        pd, pu = cube + (256, D), cube + (128, H)
        outs = [sds(up), sds(down)] * 3 + [sds((2, 1, T, D), BF16)]
        n_out = len(outs)
        outs += [sds((8, T, D), BF16), sds((4, T, D), BF16), sds((6, T, D))]
        for i in range(4):
            outs += [sds(pd, BF16), sds(pu, BF16)]
        outs += [sds((4, 256, D)), sds((4, 128, H)), sds(pd, BF16), sds(pu, BF16)]
        outs += [sds((4, 256, D)), sds((4, 64, H)), sds((4, 64, H)), sds((4, 64, H), BF16)]
        any_spec = pl.BlockSpec(memory_space=pl.ANY)
        dma = pltpu.SemaphoreType.DMA
        tok_v, hid_v = pltpu.VMEM((2 * T, D), BF16), pltpu.VMEM((2 * T, H), BF16)
        sum_d, sum_u = pltpu.VMEM((256, D), F32), pltpu.VMEM((128, H), F32)
        pair_sem = dma((2,))
        scratch = [
            tok_v, tok_v, pltpu.VMEM((D, H), BF16), pltpu.VMEM((H, D), BF16),
            hid_v, hid_v, pltpu.VMEM((2, T, D), F32),
            pltpu.VMEM((2, 256, D), BF16), pltpu.VMEM((2, 2, 128, H), BF16),
            pltpu.VMEM((4, 256, D), BF16), pltpu.VMEM((4, 128, H), BF16),
            sum_d, sum_u, sum_d, sum_u,
            dma((SEMS,)), dma((SEMS,)), dma((CHIPS,)), dma((CHIPS,)), pair_sem, pair_sem, pair_sem, dma((12,)), dma((3,)),
        ]
        res = pl.pallas_call(
            step_kernel,
            out_shape=outs,
            in_specs=[any_spec] * (5 + len(state)),
            out_specs=[any_spec] * len(outs),
            scratch_shapes=scratch,
            compiler_params=pltpu.CompilerParams(collective_id=0, has_side_effects=True, vmem_limit_bytes=66_900_000),
        )(x_saved, grad_out, x_next, w_up, w_down.reshape(2, 2, 8, 2, 256, D), *state)
        return tuple(res[:n_out])

    return jax.shard_map(device_step, mesh=mesh, in_specs=(layer_spec, tok_spec, tok_spec, rep_spec, rep_spec) + (layer_spec,) * 8, out_specs=(layer_spec,) * 6 + (tok_spec,), check_vma=False)
```

time: 1280 us -> 643 us (0.50)
  Pallas kernels: 0 us -> 606 us
  waiting for transfers between devices: 597 us -> 0 us
  matrix products: 398 us -> 0 us
  blocking collectives: 120 us -> 0 us
  other arithmetic: 106 us -> 0 us
  starting transfers between devices: 31.2 us -> 0 us
  local copies, waits for them, and re-layouts: 4.57 us -> 25.3 us
  between operations: 15.1 us -> 1.04 us
    pallas_call x0 -> x1, Pallas kernels: none -> 606 us  [device_step(): pl.pallas_call(step_kernel, out_shape=outs, in_specs=[any_spec] * (5 + le...]
    all_to_all x7 -> x0, waiting for transfers between devices: 497 us -> none  [scatter_sum(): lax.all_to_all(part.astype(jnp.bfloat16), 'fsdp', 0, 0, tiled=True)]
    dot_general x20 -> x0, matrix products: 398 us -> none  [the longest x4 104 us: forward_layer(): jnp.einsum('bsf,fd->bsd', gelu_out, w_two, preferred_element_type=jnp.flo...]
    all_to_all x1 -> x0, blocking collectives: 120 us -> none  [scatter_sum(): lax.all_to_all(part.astype(jnp.bfloat16), 'fsdp', 0, 0, tiled=True)]
    all_gather x8 -> x0, waiting for transfers between devices: 97.4 us -> none  [the longest x4 50.9 us: device_step(): lax.all_gather(new_up[0].astype(jnp.bfloat16), 'fsdp', axis=0, tiled=True)]
    reduce_sum x8 -> x0, other arithmetic: 40.2 us -> none  [scatter_sum(): jnp.sum(received.reshape((groups, -1) + received.shape[1:]), axis=0, dtyp...]
    all_to_all x7 -> x0, starting transfers between devices: 30.3 us -> none  [scatter_sum(): lax.all_to_all(part.astype(jnp.bfloat16), 'fsdp', 0, 0, tiled=True)]
    sub x4 -> x0, other arithmetic: 23.7 us -> none  [adam_update(): master = master - LEARN_RATE * (step_dir + WEIGHT_DECAY * master)]
  transfers between devices with their start and end apart: 15 -> 0, of which waited for: 10 -> 0; matrix products, arithmetic and copies ran while one was open for 35% -> 0% of each run, Pallas kernels for 0% -> 0%
where the time goes in v2:
time: 643 us; the launch traced here: 633 us
  Pallas kernels  606 us (94%)
  local copies, waits for them, and re-layouts  25.3 us (4%)
    pallas_call x1, Pallas kernels, device_step(): pl.pallas_call(step_kernel, out_shape=outs, in_specs=[any_spec] * (5 + le...  606 us
    unnamed x19, local copies, waits for them, and re-layouts  25.3 us

profile of v2, /device:TPU:0, one launch (start us, length us, event | category | flops | bytes accessed | tf_op | source)
XLA Modules:
  0.0 632.6 jit_solution(8309177076982851281)
XLA Ops:
  0.6 606.3 %shard_map.180 = (f32[2,2,64,4096]{3,2,1,0:T(8,128)}, f32[2,2,256,1024]{3,2,1,0:T(8,128)}, f32[2,2,64,4096]{3,2,1,0:T(8,128)}, f32[2,2,256,1024]{3,2,1,0:T(8,128...) custom-call(bf16[2,2,1,1024,1024]{4,3,2,1,0:T(8,128)(2,1)} %refs_0_., ...), custom_call_target="tpu_custom_call" | custom-call | tf_op jit(solution)/shard_map/pallas_call | solution.py:530
  606.9 0.0 copy-start.5
  606.9 4.8 copy.27
  611.7 0.0 copy-done.5
  611.7 0.0 copy-start.4
  611.7 2.1 copy.28
  613.9 1.6 copy-done.4
  615.4 0.0 copy-start.3
  615.4 2.1 copy.29
  617.6 1.6 copy-done.3
  619.1 0.0 copy-start.2
  619.1 2.1 copy.30
  621.3 1.6 copy-done.2
  622.8 0.0 copy-start.1
  622.8 2.1 copy.31
  625.0 1.6 copy-done.1
  626.5 0.0 copy-start
  626.5 2.1 copy.32
  628.7 1.6 copy-done
  630.2 2.0 copy.33
Async XLA Ops:
  606.9 4.8 copy-start.5
  611.7 3.7 copy-start.4
  615.4 3.7 copy-start.3
  619.1 3.7 copy-start.2
  622.8 3.7 copy-start.1
  626.5 3.7 copy-start

commit v3 on v2

--- a/solution.py
+++ b/solution.py
@@ -28,13 +28,23 @@
 TM = 256
 TF = 512
 PAIR = (0, 1)
+STREAMS = (0, 1, 2)
 QUADS = 4
+START = (0, 1)
 SEMS = 230
+TASKS = {'p': ('bk', 1), 'q': ('bk', 0), 'c': ('cb', 0), 'm': ('j3', 0), 'n': ('j3', 1)}
+TAIL = ('pqmcn', 'mpqnc')
 CHIPS = 8
 SUB = 16
+LAYERS = 4
+VMEM_CAP = 66_900_000
 STEPS = {'d': (1, 2, 3, 6, 7), 'u': (1, 2, 3, 4, 5, 6, 7)}
-MATS = {'A': (0, 1, 'd'), 'B': (0, 1, 'u'), 'C': (0, 0, 'd'), 'D': (0, 0, 'u'), 'E': (1, 1, 'd'), 'F': (1, 1, 'u'), 'G': (1, 0, 'd'), 'H': (1, 0, 'u')}
-ORDER = ('jjjjjjAjjjAjBjjjjABCjjDAjjCjEjDjjCDjFDjDBHFCEDHFBD', 'FGHBCHHFBGjjHjBAjGjjFEGHjjGjEjFjjjjEjjjjjj',)
+MATS = {}
+for s in PAIR:
+    for l in reversed(PAIR):
+        for kind in 'du':
+            MATS['ABCDEFGH'[len(MATS)]] = (s, l, kind)
+ORDER = ('jjjjjjAjjAjBjjBjCjjjDjjCjEjDjFjjjBGDEFBCDHAGBDEHDB', 'HCHDGACHBjFjHAjFGjHjFjjjGjFEjjFEjjjjj',)
 
 def adam_update(acc_part, grad_new, master, moment_one, moment_two):
     grad_mean = (acc_part + grad_new) / MICROBATCHES
@@ -47,22 +57,30 @@
     return master, moment_one, moment_two
 
 
+def mat(s, l):
+    return 2 * s + l
+
+
+def bit(n):
+    return lax.rem(n, 2)
+
+
 def jobs_of():
     for s in PAIR:
         for l in reversed(PAIR):
-            for g in range(QUADS // (1 if (s, l) == (0, 1) else 2)):
+            for g in range(3 if (s, l) == START else 2):
                 yield 'k', s, l, g
-            if l:
-                yield 'bk', s, l, 1
-                yield 'bk', s, l, 0
-            yield 'j3', s, l, 0
-            if l:
-                yield 'cb', s, l, 0
-            yield 'j3', s, l, 1
+            for token in TAIL[(s, l) == START]:
+                name, half = TASKS[token]
+                if l or name == 'j3':
+                    yield name, s, l, half
     for s in PAIR:
         for l in PAIR:
-            for name, half in (('f1', 1 - l), ('f1', l), ('f2', 1), ('f2', 0), ('cf', 0)):
-                yield name, s, l, half
+            for name, half in (('f1', 0), ('f1', 1), ('f2', 1), ('f2', 0), ('cf', 0)):
+                if name == 'f1' and half and not l:
+                    continue
+                if (s, l) != (1, 1) or name == 'f1' or half:
+                    yield name, s, l, half
 
 
 def gelu_parts(h):
@@ -80,18 +98,18 @@
     take = lambda n: [next(it) for i in range(n)]
     x_saved, grad_out, x_next, w_up, w_down = take(5)
     acc, mast, mom1, mom2 = [dict(zip('ud', take(2))) for i in range(4)]
-    nmast, nmom1, nmom2 = [dict(zip('ud', take(2))) for i in range(3)]
-    (y_out,) = take(1)
+    nmast, nmom1, nmom2 = [dict(zip('ud', take(2))) for i in STREAMS]
+    y_out, x_out, a_out = take(3)
     xr, tokr, pr = take(3)
     part, r1, r2o, r2f, r3, aw = [dict(zip('du', take(2))) for i in range(6)]
     gd, go, gx, ws = take(4)
     xv, yv, w1v, w2v, av, hv, fst, dwd, dwu = take(9)
-    sb, so, r3v = [dict(zip('du', take(2))) for i in range(3)]
+    sb, so, r3v = [dict(zip('du', take(2))) for i in STREAMS]
     ssem, rsem, w1sem, w2sem, xsem, ysem, dwsem, sbsem, msem = take(9)
 
     me = lax.axis_index('fsdp')
-    pos = {'z': lax.div(me, 8), 'y': lax.rem(lax.div(me, 4), 2), 'x': lax.rem(lax.div(me, 2), 2)}
-    core = lax.rem(me, 2)
+    pos = {'z': lax.div(me, 8), 'y': bit(lax.div(me, 4)), 'x': bit(lax.div(me, 2))}
+    core = bit(me)
     flip = {a: 1 - pos[a] for a in AXES}
     peer = {a: me + step * (1 - 2 * pos[a]) for a, step in (('z', 8), ('y', 4), ('x', 2))}
     peer['core'] = me + 1 - 2 * core
@@ -150,7 +168,7 @@
         return pl.ds(pl.multiple_of(n * size, size), size)
 
     def quad(g):
-        return lax.rem(pos['z'] + 1 + lax.div(g, 2), 2), lax.rem(pos['y'] + 1 + lax.rem(g, 2), 2)
+        return bit(flip['z'] + lax.div(g, 2)), bit(flip['y'] + g)
 
     def backward(i, g0, count, hook=None):
         def block(g, hook=None):
@@ -233,7 +251,7 @@
             rows = pl.ds(TF * e, TF)
             remote(('pr', send, e), fst.at[0, rows], pr.at[send, rows], 'core')
 
-    def f1(half):
+    def f1(half, many):
         def body(n, carry):
             ts = slab(T // TM * half + lax.div(n, H // TF), TM)
             fs = slab(lax.rem(n, H // TF), TF)
@@ -241,7 +259,7 @@
             sq, th = gelu_parts(h)
             av[ts, fs] = (h * (0.5 * (1.0 + th))).astype(BF16)
             return carry
-        lax.fori_loop(0, (T // TM) * (H // TF), body, 0)
+        lax.fori_loop(0, many * (T // TM) * (H // TF), body, 0)
 
     def combine(n_pr, base):
         cps = []
@@ -259,8 +277,8 @@
                 return carry
             lax.fori_loop(TF * e // SUB, TF * (e + 1) // SUB, body, 0)
 
-    def streams(kind):
-        return zip(range(3), COLS[kind], ORDERS)
+    def streams(kind, s):
+        return zip(STREAMS, COLS[kind], ORDERS[s:] + ORDERS[:s])
 
     last_so = {'d': None, 'u': None}
     last_gx = [None]
@@ -272,14 +290,14 @@
             cp.wait()
 
     def send_own(kind, m):
-        i = 2 * m[0] + m[1]
-        for q, (c0, n), (a, b, c) in streams(kind):
+        i = mat(*m[:2])
+        for q, (c0, n), (a, b, c) in streams(kind, m[0]):
             fix = {a: pos[a], b: flip[b]}
             remote(('r2o', m, q), cut(part[kind], i, fix, c0, n), cut(r2o[kind], i, fix, c0, n), b)
 
     def send_half(kind, m, fix, which=AXES):
-        i = 2 * m[0] + m[1]
-        for q, (c0, n), (a, b, c) in streams(kind):
+        i = mat(*m[:2])
+        for q, (c0, n), (a, b, c) in streams(kind, m[0]):
             if a in which:
                 where = {**fix, a: flip[a]}
                 key = ('r1', m, q)
@@ -288,26 +306,26 @@
 
     def service(m, step):
         s, l, kind = m
-        i = 2 * s + l
+        i = mat(s, l)
         rows, wide = ROWS[kind], WIDE[kind]
         pa, a1, a2, a3, a4 = part[kind], r1[kind], r2o[kind], r2f[kind], r3[kind]
         key = lambda name, q: (name, m, q)
         if step == 1:
-            for q, (c0, n), (a, b, c) in streams(kind):
+            for q, (c0, n), (a, b, c) in streams(kind, m[0]):
                 for k in first[key('r1', q)]:
                     recv(k)
                 fix = {a: pos[a], b: flip[b]}
                 remote(key('r2f', q), cut(a1, i, fix, c0, n), cut(a3, i, fix, c0, n), b)
         if step == 2:
             items = []
-            for q, (c0, n), (a, b, c) in streams(kind):
+            for q, (c0, n), (a, b, c) in streams(kind, m[0]):
                 recv(key('r2o', q))
                 recv(key('r2f', q))
                 fix = {a: pos[a], b: pos[b], c: flip[c]}
                 for e, src in enumerate((pa, a1, a2, a3)):
                     items.append((cut(src, i, fix, c0, n), sb[kind].at[e, :, pl.ds(c0, n)]))
             if last_so[kind] is not None:
-                for q in range(3):
+                for q in STREAMS:
                     wait_send(('r3', last_so[kind], q))
             last_so[kind] = m
             fetch(kind, items)
@@ -318,10 +336,10 @@
                 so[kind][r, :] = (v[0, r, :].astype(F32) + v[1, r, :].astype(F32)) + (v[2, r, :].astype(F32) + v[3, r, :].astype(F32))
                 return carry
             lax.fori_loop(0, rows // SUB, body, 0)
-            for q, (c0, n), (a, b, c) in streams(kind):
+            for q, (c0, n), (a, b, c) in streams(kind, m[0]):
                 remote(key('r3', q), so[kind].at[:, pl.ds(c0, n)], a4.at[i, :, pl.ds(c0, n)], c)
         if step == 3:
-            for q in range(3):
+            for q in STREAMS:
                 recv(key('r3', q))
             if kind == 'u' and last_gx[0] is not None:
                 wait_send(last_gx[0])
@@ -371,24 +389,24 @@
             recv(('ws', m))
         w = aw[kind]
         if (kind == 'd' and step == 3) or step == 5:
-            for q, (c0, n), (a, b, c) in streams(kind):
+            for q, (c0, n), (a, b, c) in streams(kind, m[0]):
                 v = cut(w, i, pos, c0, n)
                 remote(key('a1', q), v, v, c)
         if step == 6:
-            for q, (c0, n), (a, b, c) in streams(kind):
+            for q, (c0, n), (a, b, c) in streams(kind, m[0]):
                 recv(key('a1', q))
                 v = cut(w, i, {a: pos[a], b: pos[b]}, c0, n)
                 remote(key('a2', q), v, v, b)
         if step == 7:
-            for q, (c0, n), (a, b, c) in streams(kind):
+            for q, (c0, n), (a, b, c) in streams(kind, m[0]):
                 recv(key('a2', q))
                 v = cut(w, i, {a: pos[a]}, c0, n)
                 remote(key('a3', q), v, v, a)
 
-    load_x(0, x_saved.at[0, 1, 0])
-    load_w1(0, 1)
+    load_x(0, x_saved.at[START + (0,)])
+    load_w1(*START)
     load_y(0, grad_out.at[0, 0])
-    load_w2(0, 1)
+    load_w2(*START)
     barrier = pltpu.get_barrier_semaphore()
     for axis in ('x', 'y', 'z', 'core'):
         pl.semaphore_signal(barrier, inc=1, device_id=(peer[axis],), device_id_type=MESH)
@@ -406,7 +424,7 @@
             service(MATS[token], next(steps[MATS[token]]))
             continue
         name, s, l, half = next(jobs)
-        i = 2 * s + l
+        i = mat(s, l)
         nxt = following[s, l]
         own = pl.ds(0, T)
         if name == 'k':
@@ -417,7 +435,7 @@
                 load_y(1, xr.at[1])
                 ready('xb', 'yb')
             m = (s, l, 'd')
-            start = (s, l) == (0, 1)
+            start = (s, l) == START
             if half == 0:
                 ready('xa', 'ya', 'w1', 'w2')
                 if l == 0:
@@ -426,15 +444,13 @@
                 if not start:
                     ready('xb', 'yb')
             g = half if start else 2 * half
-            backward(i, g, 1 if start else 2, arrive if start and half == 0 else None)
+            many = 2 if g == 2 or not start else 1
+            backward(i, g, many, arrive if start and half == 0 else None)
             zz, yy = quad(jnp.int32(g))
-            g += 0 if start else 1
-            send_half('d', m, {'z': zz, 'y': yy} if start else {'z': zz}, 'x')
-            if g == 1:
-                send_half('d', m, {}, 'z')
-            if g == (2 if start else QUADS - 1):
-                send_half('d', m, {}, 'y')
-            if g == QUADS - 1:
+            last = g + many == QUADS
+            which = 'xy' if last else 'xyz' if half == 0 else 'xz'
+            send_half('d', m, {'z': zz} if many == 2 else {'z': zz, 'y': yy}, which)
+            if last:
                 send_own('d', m)
                 if nxt:
                     load_w2(*nxt)
@@ -461,25 +477,33 @@
             combine(s, yv)
             remote(('tk', s), yv.at[own], tokr.at[s], 'core')
         elif name == 'f1':
-            if half == 1 - l:
-                for q in range(3):
+            if half == 0:
+                for q in STREAMS:
                     recv(('a3', (s, l, 'u'), q))
                 load_new('u', i)
                 if l == 0:
                     ready('xa', 'xb')
                 ready('w1')
-            elif l:
+            else:
                 recv(('tk', 2 + s))
                 load_x(1, tokr.at[2 + s])
                 ready('xb')
-            f1(half)
+            f1(half, 1 if l else 2)
         elif name == 'f2':
             if half:
-                for q in range(3):
+                for q in STREAMS:
                     recv(('a3', (s, l, 'd'), q))
                 load_new('d', i)
                 ready('w2')
+            last = (s, l) == (1, 1)
+            if last:
+                keep = [local(xv.at[own], x_out, msem.at[0]), local(av.at[own], a_out, msem.at[1])]
             proj(half, av, 1 - half, w2v, 0, 2 + i if half else None)
+            if last:
+                for cp in keep:
+                    cp.wait()
+                for e in PAIR:
+                    recv(('pr', 2 + i, e))
         elif name == 'cf':
             if l:
                 wait_send(('tk', 2 + s))
@@ -487,13 +511,52 @@
             if l == 0:
                 remote(('tk', 2 + s), xv.at[own], tokr.at[2 + s], 'core')
             else:
-                local(xv.at[own], y_out.at[s, 0], msem.at[2]).wait()
-                if s == 0:
-                    load_x(0, x_next.at[1, 0])
-                    recv(('tok', 7))
-                    load_x(1, xr.at[7])
+                local(xv.at[own], y_out, msem.at[2]).wait()
+                load_x(0, x_next.at[1, 0])
+                recv(('tok', 7))
+                load_x(1, xr.at[7])
     for key in sends:
         wait_send(key)
+
+
+def finish(*refs):
+    states, (y0, x_in, a_in, aw, pr), outs = refs[:6], refs[6:11], refs[11:18]
+    stage_u, stage_d, yv, xv, av, wv, pv, isem, osem, lsem = refs[18:]
+    last = (LAYERS - 1,)
+    loads = [(a_in, av), (x_in, xv), (pr.at[last[0] + 2], pv)]
+    for c in range(CHIPS):
+        loads.append((aw.at[last + (c // 4, c // 2 % 2, c % 2)], wv.at[pl.ds(256 * c, 256)]))
+    loads = [pltpu.make_async_copy(src, dst, lsem.at[n]) for n, (src, dst) in enumerate(loads)]
+    moves = [(y0, yv, outs[6].at[0, 0])]
+    for n in range(6):
+        buf = (stage_u, stage_d)[n % 2]
+        for s in PAIR:
+            for l in PAIR:
+                slot = buf.at[n // 2, s, l]
+                moves.append((states[n].at[s, l], slot, outs[n].at[s, l]))
+    ins = [pltpu.make_async_copy(a, b, isem.at[n]) for n, (a, b, c) in enumerate(moves)]
+    ends = [pltpu.make_async_copy(b, c, osem.at[n]) for n, (a, b, c) in enumerate(moves)]
+    for cp in loads + ins:
+        cp.start()
+    for cp in loads:
+        cp.wait()
+    tiles = T // TM
+    for n in range(tiles):
+        rows = pl.ds(n * TM, TM)
+
+        def inner(c, carry):
+            cs = pl.ds(pl.multiple_of(c * TF, TF), TF)
+            own = dot(av[rows, :], wv[:, cs], 1, 0)
+            xv[rows, cs] = (xv[rows, cs].astype(F32) + (own + pv[rows, cs])).astype(BF16)
+            return carry
+        lax.fori_loop(0, D // TF, inner, 0)
+        for k in range(n, len(moves), tiles):
+            ins[k].wait()
+            ends[k].start()
+    out = pltpu.make_async_copy(xv, outs[6].at[1, 0], lsem.at[0])
+    out.start()
+    for cp in ends + [out]:
+        cp.wait()
 
 
 def solution(mesh):
@@ -507,12 +570,16 @@
         up, down = (2, 2, 64, 4096), (2, 2, 256, 1024)
         cube = (4, 2, 2, 2)
         pd, pu = cube + (256, D), cube + (128, H)
-        outs = [sds(up), sds(down)] * 3 + [sds((2, 1, T, D), BF16)]
-        n_out = len(outs)
-        outs += [sds((8, T, D), BF16), sds((4, T, D), BF16), sds((6, T, D))]
+        states = [sds(up), sds(down)] * 3
+        tok = sds((T, D), BF16)
+        outs = states + [tok, tok, sds((T, H), BF16)]
+        n_pr = len(outs) + 2
+        outs += [sds((CHIPS, T, D), BF16), sds((LAYERS, T, D), BF16), sds((6, T, D))]
         for i in range(4):
             outs += [sds(pd, BF16), sds(pu, BF16)]
-        outs += [sds((4, 256, D)), sds((4, 128, H)), sds(pd, BF16), sds(pu, BF16)]
+        outs += [sds((4, 256, D)), sds((4, 128, H))]
+        n_aw = len(outs)
+        outs += [sds(pd, BF16), sds(pu, BF16)]
         outs += [sds((4, 256, D)), sds((4, 64, H)), sds((4, 64, H)), sds((4, 64, H), BF16)]
         any_spec = pl.BlockSpec(memory_space=pl.ANY)
         dma = pltpu.SemaphoreType.DMA
@@ -533,8 +600,17 @@
             in_specs=[any_spec] * (5 + len(state)),
             out_specs=[any_spec] * len(outs),
             scratch_shapes=scratch,
-            compiler_params=pltpu.CompilerParams(collective_id=0, has_side_effects=True, vmem_limit_bytes=66_900_000),
+            compiler_params=pltpu.CompilerParams(collective_id=0, has_side_effects=True, vmem_limit_bytes=VMEM_CAP),
         )(x_saved, grad_out, x_next, w_up, w_down.reshape(2, 2, 8, 2, 256, D), *state)
-        return tuple(res[:n_out])
+        vm = pltpu.VMEM
+        final = pl.pallas_call(
+            finish,
+            out_shape=states + [sds((2, 1, T, D), BF16)],
+            in_specs=[any_spec] * 11,
+            out_specs=[any_spec] * 7,
+            scratch_shapes=[vm((3,) + up, F32), vm((3,) + down, F32), vm((T, D), BF16), vm((T, D), BF16), vm((T, H), BF16), vm((H, D), BF16), vm((T, D), F32), dma((32,)), dma((32,)), dma((12,))],
+            compiler_params=pltpu.CompilerParams(vmem_limit_bytes=VMEM_CAP),
+        )(*res[:9], res[n_aw], res[n_pr])
+        return tuple(final)
 
     return jax.shard_map(device_step, mesh=mesh, in_specs=(layer_spec, tok_spec, tok_spec, rep_spec, rep_spec) + (layer_spec,) * 8, out_specs=(layer_spec,) * 6 + (tok_spec,), check_vma=False)

time: 643 us -> 620 us (0.964); the launches traced: 633 us -> 619 us
  local copies, waits for them, and re-layouts: 25.3 us -> 0 us
  Pallas kernels: 606 us -> 618 us
    unnamed x19 -> x0, local copies, waits for them, and re-layouts: 25.3 us -> none
    pallas_call x0 -> x1, Pallas kernels: none -> 24.4 us  [device_step(): pl.pallas_call(finish, out_shape=states + [sds((2, 1, T, D), BF16)], in_s...]
    pallas_call x1, Pallas kernels: 606 us -> 593 us  [device_step(): pl.pallas_call(step_kernel, out_shape=outs, in_specs=[any_spec] * (5 + le...]
where the time goes in v3:
time: 620 us; the launch traced here: 619 us
  Pallas kernels  618 us (100%)
    pallas_call x1, Pallas kernels, device_step(): pl.pallas_call(step_kernel, out_shape=outs, in_specs=[any_spec] * (5 + le...  593 us
    pallas_call x1, Pallas kernels, device_step(): pl.pallas_call(finish, out_shape=states + [sds((2, 1, T, D), BF16)], in_s...  24.4 us

profile of v3, /device:TPU:0, one launch (start us, length us, event | category | flops | bytes accessed | tf_op | source)
XLA Modules:
  0.0 618.7 jit_solution(16750616790228014752)
XLA Ops:
  0.6 593.5 %shard_map.180 = (f32[2,2,64,4096]{3,2,1,0:T(8,128)}, f32[2,2,256,1024]{3,2,1,0:T(8,128)}, f32[2,2,64,4096]{3,2,1,0:T(8,128)}, f32[2,2,256,1024]{3,2,1,0:T(8,128...) custom-call(bf16[2,2,1,1024,1024]{4,3,2,1,0:T(8,128)(2,1)} %refs_0_., ...), custom_call_target="tpu_custom_call" | custom-call | tf_op jit(solution)/shard_map/pallas_call | solution.py:597
  594.1 24.4 %shard_map.181 = (f32[2,2,64,4096]{3,2,1,0:T(8,128)}, f32[2,2,256,1024]{3,2,1,0:T(8,128)}, f32[2,2,64,4096]{3,2,1,0:T(8,128)}, f32[2,2,256,1024]{3,2,1,0:T(8,128...) custom-call(f32[2,2,64,4096]{3,2,1,0:T(8,128)} %get-tuple-element.18.refs_0_, ...), custom_call_target="tpu_custom_call" | custom-call | tf_op jit(solution)/shard_map/pallas_call | solution.py:606

commit v4 on v3

--- a/solution.py
+++ b/solution.py
@@ -31,7 +31,8 @@
 STREAMS = (0, 1, 2)
 QUADS = 4
 START = (0, 1)
-SEMS = 230
+LAST = (1, 1, 'd')
+SEMS = 240
 TASKS = {'p': ('bk', 1), 'q': ('bk', 0), 'c': ('cb', 0), 'm': ('j3', 0), 'n': ('j3', 1)}
 TAIL = ('pqmcn', 'mpqnc')
 CHIPS = 8
@@ -44,7 +45,7 @@
     for l in reversed(PAIR):
         for kind in 'du':
             MATS['ABCDEFGH'[len(MATS)]] = (s, l, kind)
-ORDER = ('jjjjjjAjjAjBjjBjCjjjDjjCjEjDjFjjjBGDEFBCDHAGBDEHDB', 'HCHDGACHBjFjHAjFGjHjFjjjGjFEjjFEjjjjj',)
+ORDER = ('jjjjjjAjjAjBjBjCjjCjjjDjEjjjDFjjEjDBDCGFBDHAGDBECH', 'FBAFDHHCGHBjHjGAjjjFHjjGFEjjjFjEjjjjj',)
 
 def adam_update(acc_part, grad_new, master, moment_one, moment_two):
     grad_mean = (acc_part + grad_new) / MICROBATCHES
@@ -79,7 +80,7 @@
             for name, half in (('f1', 0), ('f1', 1), ('f2', 1), ('f2', 0), ('cf', 0)):
                 if name == 'f1' and half and not l:
                     continue
-                if (s, l) != (1, 1) or name == 'f1' or half:
+                if (s, l) != LAST[:2] or name == 'f1' or (name, half) == ('f2', 1):
                     yield name, s, l, half
 
 
@@ -99,7 +100,7 @@
     x_saved, grad_out, x_next, w_up, w_down = take(5)
     acc, mast, mom1, mom2 = [dict(zip('ud', take(2))) for i in range(4)]
     nmast, nmom1, nmom2 = [dict(zip('ud', take(2))) for i in STREAMS]
-    y_out, x_out, a_out = take(3)
+    y_out, x_out, a_out, a_far, w_far = take(5)
     xr, tokr, pr = take(3)
     part, r1, r2o, r2f, r3, aw = [dict(zip('du', take(2))) for i in range(6)]
     gd, go, gx, ws = take(4)
@@ -277,8 +278,9 @@
                 return carry
             lax.fori_loop(TF * e // SUB, TF * (e + 1) // SUB, body, 0)
 
-    def streams(kind, s):
-        return zip(STREAMS, COLS[kind], ORDERS[s:] + ORDERS[:s])
+    def streams(kind, m):
+        r = mat(*m[:2]) % len(ORDERS)
+        return zip(STREAMS, COLS[kind], ORDERS[r:] + ORDERS[:r])
 
     last_so = {'d': None, 'u': None}
     last_gx = [None]
@@ -291,18 +293,25 @@
 
     def send_own(kind, m):
         i = mat(*m[:2])
-        for q, (c0, n), (a, b, c) in streams(kind, m[0]):
+        for q, (c0, n), (a, b, c) in streams(kind, m):
             fix = {a: pos[a], b: flip[b]}
             remote(('r2o', m, q), cut(part[kind], i, fix, c0, n), cut(r2o[kind], i, fix, c0, n), b)
 
     def send_half(kind, m, fix, which=AXES):
         i = mat(*m[:2])
-        for q, (c0, n), (a, b, c) in streams(kind, m[0]):
+        for q, (c0, n), (a, b, c) in streams(kind, m):
             if a in which:
                 where = {**fix, a: flip[a]}
                 key = ('r1', m, q)
                 first.setdefault(key, []).append(key + (len(first.get(key, ())),))
                 remote(first[key][-1], cut(part[kind], i, where, c0, n), cut(r1[kind], i, where, c0, n), a)
+
+    def far_half(fix, q, c0, n):
+        i = mat(*LAST[:2])
+        part_of = lambda ref: ref.at[tuple(fix.get(a, slice(None)) for a in AXES) + (slice(None), pl.ds(c0, n))]
+        key = ('far', q)
+        first.setdefault(key, []).append(key + (len(first.get(key, ())),))
+        remote(first[key][-1], cut(aw['d'], i, fix, c0, n), part_of(w_far), 'core')
 
     def service(m, step):
         s, l, kind = m
@@ -311,14 +320,14 @@
         pa, a1, a2, a3, a4 = part[kind], r1[kind], r2o[kind], r2f[kind], r3[kind]
         key = lambda name, q: (name, m, q)
         if step == 1:
-            for q, (c0, n), (a, b, c) in streams(kind, m[0]):
+            for q, (c0, n), (a, b, c) in streams(kind, m):
                 for k in first[key('r1', q)]:
                     recv(k)
                 fix = {a: pos[a], b: flip[b]}
                 remote(key('r2f', q), cut(a1, i, fix, c0, n), cut(a3, i, fix, c0, n), b)
         if step == 2:
             items = []
-            for q, (c0, n), (a, b, c) in streams(kind, m[0]):
+            for q, (c0, n), (a, b, c) in streams(kind, m):
                 recv(key('r2o', q))
                 recv(key('r2f', q))
                 fix = {a: pos[a], b: pos[b], c: flip[c]}
@@ -336,7 +345,7 @@
                 so[kind][r, :] = (v[0, r, :].astype(F32) + v[1, r, :].astype(F32)) + (v[2, r, :].astype(F32) + v[3, r, :].astype(F32))
                 return carry
             lax.fori_loop(0, rows // SUB, body, 0)
-            for q, (c0, n), (a, b, c) in streams(kind, m[0]):
+            for q, (c0, n), (a, b, c) in streams(kind, m):
                 remote(key('r3', q), so[kind].at[:, pl.ds(c0, n)], a4.at[i, :, pl.ds(c0, n)], c)
         if step == 3:
             for q in STREAMS:
@@ -389,19 +398,21 @@
             recv(('ws', m))
         w = aw[kind]
         if (kind == 'd' and step == 3) or step == 5:
-            for q, (c0, n), (a, b, c) in streams(kind, m[0]):
+            for q, (c0, n), (a, b, c) in streams(kind, m):
                 v = cut(w, i, pos, c0, n)
                 remote(key('a1', q), v, v, c)
         if step == 6:
-            for q, (c0, n), (a, b, c) in streams(kind, m[0]):
+            for q, (c0, n), (a, b, c) in streams(kind, m):
                 recv(key('a1', q))
                 v = cut(w, i, {a: pos[a], b: pos[b]}, c0, n)
                 remote(key('a2', q), v, v, b)
         if step == 7:
-            for q, (c0, n), (a, b, c) in streams(kind, m[0]):
+            for q, (c0, n), (a, b, c) in streams(kind, m):
                 recv(key('a2', q))
                 v = cut(w, i, {a: pos[a]}, c0, n)
                 remote(key('a3', q), v, v, a)
+                if m == LAST:
+                    far_half({a: pos[a]}, q, c0, n)
 
     load_x(0, x_saved.at[START + (0,)])
     load_w1(*START)
@@ -414,7 +425,7 @@
     toks = [x_saved.at[0, 1, 0], grad_out.at[0, 0], x_saved.at[0, 0, 0], x_saved.at[1, 1, 0], grad_out.at[1, 0], x_saved.at[1, 0, 0], x_next.at[0, 0], x_next.at[1, 0]]
     xid = {(0, 1): 0, (0, 0): 2, (1, 1): 3, (1, 0): 5}
     for n, src in enumerate(toks):
-        remote(('tok', n), src, xr.at[n], 'core')
+        remote(('tok', n), src, (xv, yv)[n].at[pl.ds(T, T)] if n < 2 else xr.at[n], 'core')
 
     following = {(0, 1): (0, 0), (0, 0): (1, 1), (1, 1): (1, 0), (1, 0): None}
     jobs = jobs_of()
@@ -429,11 +440,8 @@
         own = pl.ds(0, T)
         if name == 'k':
             def arrive():
-                recv(('tok', 0))
-                load_x(1, xr.at[0])
-                recv(('tok', 1))
-                load_y(1, xr.at[1])
-                ready('xb', 'yb')
+                for n in PAIR:
+                    recv(('tok', n))
             m = (s, l, 'd')
             start = (s, l) == START
             if half == 0:
@@ -489,21 +497,28 @@
                 load_x(1, tokr.at[2 + s])
                 ready('xb')
             f1(half, 1 if l else 2)
+            if (s, l) == LAST[:2]:
+                if half:
+                    remote('a_far', av.at[pl.ds(T, T)], a_far, 'core')
+                else:
+                    keep = [local(xv.at[own], x_out, msem.at[0]), local(av.at[own], a_out, msem.at[1])]
+        elif name == 'f2' and (s, l) == LAST[:2]:
+            for q, (c0, n), (a, b, c) in streams('d', LAST):
+                recv(('a3', LAST, q))
+                far_half({a: flip[a]}, q, c0, n)
+            for cp in keep:
+                cp.wait()
+            for q in STREAMS:
+                for k in first['far', q]:
+                    recv(k)
+            recv('a_far')
         elif name == 'f2':
             if half:
                 for q in STREAMS:
                     recv(('a3', (s, l, 'd'), q))
                 load_new('d', i)
                 ready('w2')
-            last = (s, l) == (1, 1)
-            if last:
-                keep = [local(xv.at[own], x_out, msem.at[0]), local(av.at[own], a_out, msem.at[1])]
             proj(half, av, 1 - half, w2v, 0, 2 + i if half else None)
-            if last:
-                for cp in keep:
-                    cp.wait()
-                for e in PAIR:
-                    recv(('pr', 2 + i, e))
         elif name == 'cf':
             if l:
                 wait_send(('tk', 2 + s))
@@ -520,12 +535,14 @@
 
 
 def finish(*refs):
-    states, (y0, x_in, a_in, aw, pr), outs = refs[:6], refs[6:11], refs[11:18]
-    stage_u, stage_d, yv, xv, av, wv, pv, isem, osem, lsem = refs[18:]
+    states, (y0, x_in, a_in, a_far, w_far, aw), outs = refs[:6], refs[6:12], refs[12:19]
+    stage_u, stage_d, yv, xv, av, wv, isem, osem, lsem = refs[19:]
     last = (LAYERS - 1,)
-    loads = [(a_in, av), (x_in, xv), (pr.at[last[0] + 2], pv)]
+    loads = [(x_in, xv), (a_in, av.at[0]), (a_far, av.at[1])]
     for c in range(CHIPS):
-        loads.append((aw.at[last + (c // 4, c // 2 % 2, c % 2)], wv.at[pl.ds(256 * c, 256)]))
+        spot = (c // 4, c // 2 % 2, c % 2)
+        for e, src in enumerate((aw.at[last + spot], w_far.at[spot])):
+            loads.append((src, wv.at[e, pl.ds(256 * c, 256)]))
     loads = [pltpu.make_async_copy(src, dst, lsem.at[n]) for n, (src, dst) in enumerate(loads)]
     moves = [(y0, yv, outs[6].at[0, 0])]
     for n in range(6):
@@ -540,17 +557,19 @@
         cp.start()
     for cp in loads:
         cp.wait()
-    tiles = T // TM
-    for n in range(tiles):
-        rows = pl.ds(n * TM, TM)
+    def tile(n, carry):
+        rows = pl.ds(pl.multiple_of(n * TM, TM), TM)
 
         def inner(c, carry):
             cs = pl.ds(pl.multiple_of(c * TF, TF), TF)
-            own = dot(av[rows, :], wv[:, cs], 1, 0)
-            xv[rows, cs] = (xv[rows, cs].astype(F32) + (own + pv[rows, cs])).astype(BF16)
+            mlp = dot(av[0, rows, :], wv[0, :, cs], 1, 0) + dot(av[1, rows, :], wv[1, :, cs], 1, 0)
+            xv[rows, cs] = (xv[rows, cs].astype(F32) + mlp).astype(BF16)
             return carry
-        lax.fori_loop(0, D // TF, inner, 0)
-        for k in range(n, len(moves), tiles):
+        return lax.fori_loop(0, D // TF, inner, carry)
+    group = T // TM // len(PAIR)
+    for g in PAIR:
+        lax.fori_loop(group * g, group * (g + 1), tile, 0)
+        for k in range(g, len(moves), len(PAIR)):
             ins[k].wait()
             ends[k].start()
     out = pltpu.make_async_copy(xv, outs[6].at[1, 0], lsem.at[0])
@@ -572,8 +591,9 @@
         pd, pu = cube + (256, D), cube + (128, H)
         states = [sds(up), sds(down)] * 3
         tok = sds((T, D), BF16)
-        outs = states + [tok, tok, sds((T, H), BF16)]
-        n_pr = len(outs) + 2
+        hid = sds((T, H), BF16)
+        outs = states + [tok, tok, hid, hid, sds((2, 2, 2, 256, D), BF16)]
+        n_main = len(outs)
         outs += [sds((CHIPS, T, D), BF16), sds((LAYERS, T, D), BF16), sds((6, T, D))]
         for i in range(4):
             outs += [sds(pd, BF16), sds(pu, BF16)]
@@ -606,11 +626,11 @@
         final = pl.pallas_call(
             finish,
             out_shape=states + [sds((2, 1, T, D), BF16)],
-            in_specs=[any_spec] * 11,
+            in_specs=[any_spec] * 12,
             out_specs=[any_spec] * 7,
-            scratch_shapes=[vm((3,) + up, F32), vm((3,) + down, F32), vm((T, D), BF16), vm((T, D), BF16), vm((T, H), BF16), vm((H, D), BF16), vm((T, D), F32), dma((32,)), dma((32,)), dma((12,))],
+            scratch_shapes=[vm((3,) + up, F32), vm((3,) + down, F32), vm((T, D), BF16), vm((T, D), BF16), vm((2, T, H), BF16), vm((2, H, D), BF16), dma((32,)), dma((32,)), dma((32,))],
             compiler_params=pltpu.CompilerParams(vmem_limit_bytes=VMEM_CAP),
-        )(*res[:9], res[n_aw], res[n_pr])
+        )(*res[:n_main], res[n_aw])
         return tuple(final)
 
     return jax.shard_map(device_step, mesh=mesh, in_specs=(layer_spec, tok_spec, tok_spec, rep_spec, rep_spec) + (layer_spec,) * 8, out_specs=(layer_spec,) * 6 + (tok_spec,), check_vma=False)

time: 620 us -> 618 us (level)
    pallas_call x1, Pallas kernels: 593 us -> 585 us  [device_step(): pl.pallas_call(step_kernel, out_shape=outs, in_specs=[any_spec] * (5 + le...]
where the time goes in v4:
time: 618 us; the launch traced here: 616 us
  Pallas kernels  615 us (100%)
    pallas_call x1, Pallas kernels, device_step(): pl.pallas_call(step_kernel, out_shape=outs, in_specs=[any_spec] * (5 + le...  585 us
    pallas_call x1, Pallas kernels, device_step(): pl.pallas_call(finish, out_shape=states + [sds((2, 1, T, D), BF16)], in_s...  30.4 us

profile of v4, /device:TPU:0, one launch (start us, length us, event | category | flops | bytes accessed | tf_op | source)
XLA Modules:
  0.0 616.1 jit_solution(5273166639742917098)
XLA Ops:
  0.6 584.8 %shard_map.180 = (f32[2,2,64,4096]{3,2,1,0:T(8,128)}, f32[2,2,256,1024]{3,2,1,0:T(8,128)}, f32[2,2,64,4096]{3,2,1,0:T(8,128)}, f32[2,2,256,1024]{3,2,1,0:T(8,128...) custom-call(bf16[2,2,1,1024,1024]{4,3,2,1,0:T(8,128)(2,1)} %refs_0_., ...), custom_call_target="tpu_custom_call" | custom-call | tf_op jit(solution)/shard_map/pallas_call | solution.py:617
  585.5 30.4 %shard_map.181 = (f32[2,2,64,4096]{3,2,1,0:T(8,128)}, f32[2,2,256,1024]{3,2,1,0:T(8,128)}, f32[2,2,64,4096]{3,2,1,0:T(8,128)}, f32[2,2,256,1024]{3,2,1,0:T(8,128...) custom-call(f32[2,2,64,4096]{3,2,1,0:T(8,128)} %get-tuple-element.19.refs_0_, ...), custom_call_target="tpu_custom_call" | custom-call | tf_op jit(solution)/shard_map/pallas_call | solution.py:626

commit v5 on v4

--- a/solution.py
+++ b/solution.py
@@ -558,18 +558,19 @@
     for cp in loads:
         cp.wait()
     def tile(n, carry):
-        rows = pl.ds(pl.multiple_of(n * TM, TM), TM)
+        rows = pl.ds(n * TM, TM)
 
         def inner(c, carry):
-            cs = pl.ds(pl.multiple_of(c * TF, TF), TF)
+            cs = pl.ds(pl.multiple_of(c * TM, TM), TM)
             mlp = dot(av[0, rows, :], wv[0, :, cs], 1, 0) + dot(av[1, rows, :], wv[1, :, cs], 1, 0)
             xv[rows, cs] = (xv[rows, cs].astype(F32) + mlp).astype(BF16)
             return carry
-        return lax.fori_loop(0, D // TF, inner, carry)
-    group = T // TM // len(PAIR)
-    for g in PAIR:
-        lax.fori_loop(group * g, group * (g + 1), tile, 0)
-        for k in range(g, len(moves), len(PAIR)):
+        return lax.fori_loop(0, D // TM, inner, carry)
+    tiles = T // TM
+    share = len(moves) // tiles
+    for n in range(tiles):
+        tile(n, 0)
+        for k in range(share * n, len(moves) if n == tiles - 1 else share * n + share):
             ins[k].wait()
             ends[k].start()
     out = pltpu.make_async_copy(xv, outs[6].at[1, 0], lsem.at[0])

time: 618 us -> 618 us (level)
  no operation moved by 1% of the time
where the time goes in v5:
time: 618 us; the launch traced here: 617 us
  Pallas kernels  616 us (100%)
    pallas_call x1, Pallas kernels, device_step(): pl.pallas_call(step_kernel, out_shape=outs, in_specs=[any_spec] * (5 + le...  585 us
    pallas_call x1, Pallas kernels, device_step(): pl.pallas_call(finish, out_shape=states + [sds((2, 1, T, D), BF16)], in_s...  30.9 us

profile of v5, /device:TPU:0, one launch (start us, length us, event | category | flops | bytes accessed | tf_op | source)
XLA Modules:
  0.0 616.6 jit_solution(4917814552038065600)
XLA Ops:
  0.6 584.8 %shard_map.180 = (f32[2,2,64,4096]{3,2,1,0:T(8,128)}, f32[2,2,256,1024]{3,2,1,0:T(8,128)}, f32[2,2,64,4096]{3,2,1,0:T(8,128)}, f32[2,2,256,1024]{3,2,1,0:T(8,128...) custom-call(bf16[2,2,1,1024,1024]{4,3,2,1,0:T(8,128)(2,1)} %refs_0_., ...), custom_call_target="tpu_custom_call" | custom-call | tf_op jit(solution)/shard_map/pallas_call | solution.py:618
  585.5 30.9 %shard_map.181 = (f32[2,2,64,4096]{3,2,1,0:T(8,128)}, f32[2,2,256,1024]{3,2,1,0:T(8,128)}, f32[2,2,64,4096]{3,2,1,0:T(8,128)}, f32[2,2,256,1024]{3,2,1,0:T(8,128...) custom-call(f32[2,2,64,4096]{3,2,1,0:T(8,128)} %get-tuple-element.19.refs_0_, ...), custom_call_target="tpu_custom_call" | custom-call | tf_op jit(solution)/shard_map/pallas_call | solution.py:627

commit v6 on v5

--- a/solution.py
+++ b/solution.py
@@ -553,10 +553,12 @@
                 moves.append((states[n].at[s, l], slot, outs[n].at[s, l]))
     ins = [pltpu.make_async_copy(a, b, isem.at[n]) for n, (a, b, c) in enumerate(moves)]
     ends = [pltpu.make_async_copy(b, c, osem.at[n]) for n, (a, b, c) in enumerate(moves)]
-    for cp in loads + ins:
+    for cp in loads:
         cp.start()
     for cp in loads:
         cp.wait()
+    for cp in ins:
+        cp.start()
     def tile(n, carry):
         rows = pl.ds(n * TM, TM)
 

time: 618 us -> 613 us (level)
  no operation moved by 1% of the time
where the time goes in v6:
time: 613 us; the launch traced here: 612 us
  Pallas kernels  611 us (100%)
    pallas_call x1, Pallas kernels, device_step(): pl.pallas_call(step_kernel, out_shape=outs, in_specs=[any_spec] * (5 + le...  585 us
    pallas_call x1, Pallas kernels, device_step(): pl.pallas_call(finish, out_shape=states + [sds((2, 1, T, D), BF16)], in_s...  25.9 us

profile of v6, /device:TPU:0, one launch (start us, length us, event | category | flops | bytes accessed | tf_op | source)
XLA Modules:
  0.0 611.6 jit_solution(12990890400555567793)
XLA Ops:
  0.6 584.8 %shard_map.180 = (f32[2,2,64,4096]{3,2,1,0:T(8,128)}, f32[2,2,256,1024]{3,2,1,0:T(8,128)}, f32[2,2,64,4096]{3,2,1,0:T(8,128)}, f32[2,2,256,1024]{3,2,1,0:T(8,128...) custom-call(bf16[2,2,1,1024,1024]{4,3,2,1,0:T(8,128)(2,1)} %refs_0_., ...), custom_call_target="tpu_custom_call" | custom-call | tf_op jit(solution)/shard_map/pallas_call | solution.py:620
  585.5 25.9 %shard_map.181 = (f32[2,2,64,4096]{3,2,1,0:T(8,128)}, f32[2,2,256,1024]{3,2,1,0:T(8,128)}, f32[2,2,64,4096]{3,2,1,0:T(8,128)}, f32[2,2,256,1024]{3,2,1,0:T(8,128...) custom-call(f32[2,2,64,4096]{3,2,1,0:T(8,128)} %get-tuple-element.19.refs_0_, ...), custom_call_target="tpu_custom_call" | custom-call | tf_op jit(solution)/shard_map/pallas_call | solution.py:629
